TPU v7x, 768 devices: a whole 4x8x12 slice. The times are simulated.
768 devices in a mesh: space: 24 (over x, z_lo), batch: 32 (over z_hi, y, core).
Axes of the slice: x: 4, y: 8, z: 12 (z_hi: 2, z_lo: 6; z = z_hi * 6 + z_lo), core: 2. Of those that a mesh axis runs over, the one named last changes fastest.
Arguments:
- pre_act: bfloat16 [32, 64, 24, 8, 128], P('batch', None, 'space'), may hold values from -6 to 6
- grad_out: bfloat16 [32, 128, 24, 8, 128], P('batch', None, 'space'), may hold values from -6 to 6
- weight: bfloat16 [27, 64, 128], replicated, may hold values from -0.109375 to 0.109375
Outputs:
- grad_in: bfloat16 [32, 64, 24, 8, 128], P('batch', None, 'space')
- weight_grad: float32 [221184], P(('space', 'batch'))
All inputs are finite; a program needn't handle non-finite values.
Results may differ from a plain program's by a relative error of at most 0.001.
Values may be sent and summed in bfloat16 or wider, within the bound.
No kernel may reach another device: no remote copies, remote signals or barrier semaphores. Data moves between devices by JAX's collectives and lax.ppermute only.
A program may use at most 32 MiB of HBM per device.

v0:
```python
import jax
import jax.numpy as jnp
from jax import lax
from jax.sharding import PartitionSpec as P

slope = 0.3


def padded(block, sides, width):
    for axis, dim in sides:
        count = lax.axis_size(axis)
        forward = [(i, i + 1) for i in range(count - 1)]
        backward = [(target, source) for source, target in forward]
        low = lax.ppermute(
            lax.slice_in_dim(block, block.shape[dim] - width, None, axis=dim), axis, forward
        )
        high = lax.ppermute(lax.slice_in_dim(block, 0, width, axis=dim), axis, backward)
        block = jnp.concatenate([low, block, high], axis=dim)
    return block


def split_up(x, dim, size):
    dims = x.shape
    pieces = x.reshape(*dims[:dim], size, dims[dim] // size, *dims[dim + 1 :])
    return jnp.moveaxis(pieces, dim, 0)


def summed_on_arrival(x, axis, dim):
    size = lax.axis_size(axis)
    pieces = lax.all_to_all(split_up(x, dim, size), axis, 0, 0, tiled=True)
    return jnp.sum(pieces, axis=0)


def leaky(values):
    return jnp.where(values > 0, values, slope * values)


def on_device(pre_act, grad_out, weight):
    local_x = pre_act.shape[2]
    local_y = pre_act.shape[3]
    local_z = pre_act.shape[4]
    count = (
        pre_act.shape[0]
        * lax.axis_size("batch")
        * local_x
        * lax.axis_size("space")
        * local_y
        * local_z
    )
    factor = 1.0 / jnp.sqrt(jnp.float32(count))
    act_float = pre_act.astype(jnp.float32)
    yz_pad = ((0, 0), (0, 0), (0, 0), (1, 1), (1, 1))
    grad_hidden = jnp.zeros(pre_act.shape, jnp.float32)
    tap_grads = []
    joined = jnp.concatenate([pre_act, grad_out], axis=1)
    widened = padded(joined, (("space", 2),), 1)
    in_chan = pre_act.shape[1]
    hidden_pad = jnp.pad(
        leaky(widened[:, :in_chan].astype(jnp.float32)).astype(jnp.bfloat16), yz_pad
    )
    grad_pad = jnp.pad(widened[:, in_chan:], yz_pad)
    for tap in range(27):
        shift_x = tap // 9 - 1
        shift_y = tap // 3 % 3 - 1
        shift_z = tap % 3 - 1
        window = grad_pad[
            :,
            :,
            1 - shift_x : 1 - shift_x + local_x,
            1 - shift_y : 1 - shift_y + local_y,
            1 - shift_z : 1 - shift_z + local_z,
        ]
        grad_hidden = grad_hidden + jnp.einsum(
            "ic,scxyz->sixyz", weight[tap], window, preferred_element_type=jnp.float32
        )
        moved = hidden_pad[
            :,
            :,
            1 + shift_x : 1 + shift_x + local_x,
            1 + shift_y : 1 + shift_y + local_y,
            1 + shift_z : 1 + shift_z + local_z,
        ]
        tap_grads.append(
            jnp.einsum("sixyz,scxyz->ic", moved, grad_out, preferred_element_type=jnp.float32)
        )
    grad_in = (grad_hidden * jnp.where(act_float > 0, 1.0, slope)).astype(jnp.bfloat16)
    partial_sum = (jnp.stack(tap_grads) * factor).reshape(-1)
    space_part = summed_on_arrival(partial_sum, "space", 0)
    weight_grad = summed_on_arrival(space_part, "batch", 0)
    return (grad_in, weight_grad)


def solution(mesh):
    return jax.shard_map(
        on_device,
        mesh=mesh,
        in_specs=(
            P("batch", None, "space", None, None),
            P("batch", None, "space", None, None),
            P(),
        ),
        out_specs=(P("batch", None, "space", None, None), P(("space", "batch"))),
        check_vma=False,
    )
```

profile of v0, /device:TPU:1, one launch (start us, length us, event | category | flops | bytes accessed | tf_op | source)
XLA Modules:
  0.0 119.9 jit_solution(8923904157386350841)
XLA Ops:
  0.6 0.9 copy_dynamic-update-slice_fusion.1
  1.6 1.0 copy_dynamic-update-slice_fusion
  2.6 1.3 %collective-permute-start.1 = (bf16[1,192,1,8,128]{4,1,3,2,0:T(8,128)(2,1)S(1)}, bf16[1,192,1,8,128]{4,1,3,2,0:T(8,128)(2,1)S(1)}, u32[]{:S(2)}, u32[]{:S(2)}) collective-permute-start(bf16[1,192,1,8,128]{4,1,3,2,0:T(8,128)(2,1)S(1)} %copy_dynamic-update-slice_fusion), channel_id=1, source_target_pairs={{32,0},{64,32},{96,64},{128,96},{160,128},{192,160},{224,192},{256... | collective-permute-start | bytes 1179656 | tf_op jit(solution)/shard_map/ppermute | solution.py:17
  3.9 5.5 %collective-permute-start = (bf16[1,192,1,8,128]{4,1,3,2,0:T(8,128)(2,1)S(1)}, bf16[1,192,1,8,128]{4,1,3,2,0:T(8,128)(2,1)S(1)}, u32[]{:S(2)}, u32[]{:S(2)}) collective-permute-start(bf16[1,192,1,8,128]{4,1,3,2,0:T(8,128)(2,1)S(1)} %copy_dynamic-update-slice_fusion), channel_id=1, source_target_pairs={{0,32},{32,64},{64,96},{96,128},{128,160},{160,192},{192,224},{224... | collective-permute-start | bytes 1179656 | tf_op jit(solution)/shard_map/ppermute | solution.py:14
  9.4 3.2 %collective-permute-done.1 = bf16[1,192,1,8,128]{4,1,3,2,0:T(8,128)(2,1)S(1)} collective-permute-done((bf16[1,192,1,8,128]{4,1,3,2,0:T(8,128)(2,1)S(1)}, bf16[1,192,1,8,128]{4,1,3,2,0:T(8,128)(2,1)S(1)}, u32[]{:S(2)}, u32[]{:S(2)}) %collective-permute-start.1) | collective-permute-done | bytes 393248 | tf_op jit(solution)/shard_map/ppermute | solution.py:17
  12.6 1.5 %collective-permute-done = bf16[1,192,1,8,128]{4,1,3,2,0:T(8,128)(2,1)S(1)} collective-permute-done((bf16[1,192,1,8,128]{4,1,3,2,0:T(8,128)(2,1)S(1)}, bf16[1,192,1,8,128]{4,1,3,2,0:T(8,128)(2,1)S(1)}, u32[]{:S(2)}, u32[]{:S(2)}) %collective-permute-start) | collective-permute-done | bytes 393248 | tf_op jit(solution)/shard_map/ppermute | solution.py:14
  14.2 0.9 copy-done.2
  15.4 0.3 fusion.90
  15.6 0.3 convolution_add_fusion.13
  15.9 0.3 convolution_add_fusion.12
  16.2 0.3 convolution_add_fusion.11
  16.6 0.3 convolution_add_fusion.9
  17.1 0.3 convolution_add_fusion.7
  17.4 0.3 convolution_add_fusion.6
  18.1 0.3 convolution_add_fusion.3
  18.4 0.4 copy-done
  25.6 1.0 broadcast_multiply_fusion
  26.6 26.1 %all-to-all-start = ((f32[24,1,9216]{2,1,0:T(1,128)}), f32[24,1,9216]{2,1,0:T(1,128)S(1)}, u32[]{:S(2)}, u32[]{:S(2)}) async-start(f32[24,1,9216]{2,1,0:T(1,128)} %bitcast.185), calls=%async_computation | async-start | bytes 1769472 | tf_op jit(solution)/shard_map/all_to_all | solution.py:30
  52.9 0.3 convolution_bitcast_fusion.3
  53.2 0.3 convolution_add_fusion.1
  53.5 0.3 fusion.14
  53.8 0.3 fusion.12
  54.8 0.3 fusion.8
  55.2 0.3 fusion.5
  55.7 26.3 %all-to-all-done = f32[24,1,9216]{2,1,0:T(1,128)S(1)} async-done(((f32[24,1,9216]{2,1,0:T(1,128)}), f32[24,1,9216]{2,1,0:T(1,128)S(1)}, u32[]{:S(2)}, u32[]{:S(2)}) %all-to-all-start) | async-done | bytes 884768 | tf_op jit(solution)/shard_map/all_to_all | solution.py:30
  82.0 0.5 reduce_sum.18
  82.5 0.7 all_to_all.11
  83.2 21.8 %all-to-all-start.1 = ((f32[32,1,288]{2,1,0:T(1,128)}), f32[32,1,288]{2,1,0:T(1,128)S(1)}, u32[]{:S(2)}, u32[]{:S(2)}) async-start(f32[32,1,288]{2,1,0:T(1,128)} %all_to_all.11), calls=%async_computation.1 | async-start | bytes 98304 | tf_op jit(solution)/shard_map/all_to_all | solution.py:30
  105.1 0.3 fusion.15
  105.4 0.7 copy.136
  106.1 13.2 %all-to-all-done.1 = f32[32,1,288]{2,1,0:T(1,128)S(1)} async-done(((f32[32,1,288]{2,1,0:T(1,128)}), f32[32,1,288]{2,1,0:T(1,128)S(1)}, u32[]{:S(2)}, u32[]{:S(2)}) %all-to-all-start.1) | async-done | bytes 36896 | tf_op jit(solution)/shard_map/all_to_all | solution.py:30
  119.3 0.6 reduce_sum.19
  (46 shorter events, 9.0 us)
Async XLA Ops:
  2.6 10.0 %collective-permute-start.1 = (bf16[1,192,1,8,128]{4,1,3,2,0:T(8,128)(2,1)S(1)}, bf16[1,192,1,8,128]{4,1,3,2,0:T(8,128)(2,1)S(1)}, u32[]{:S(2)}, u32[]{:S(2)}) collective-permute-start(bf16[1,192,1,8,128]{4,1,3,2,0:T(8,128)(2,1)S(1)} %copy_dynamic-update-slice_fusion), channel_id=1, source_target_pairs={{32,0},{64,32},{96,64},{128,96},{160,128},{192,160},{224,192},{256... | collective-permute-start | bytes 1179656 | tf_op jit(solution)/shard_map/ppermute | solution.py:17
  3.9 10.2 %collective-permute-start = (bf16[1,192,1,8,128]{4,1,3,2,0:T(8,128)(2,1)S(1)}, bf16[1,192,1,8,128]{4,1,3,2,0:T(8,128)(2,1)S(1)}, u32[]{:S(2)}, u32[]{:S(2)}) collective-permute-start(bf16[1,192,1,8,128]{4,1,3,2,0:T(8,128)(2,1)S(1)} %copy_dynamic-update-slice_fusion), channel_id=1, source_target_pairs={{0,32},{32,64},{64,96},{96,128},{128,160},{160,192},{192,224},{224... | collective-permute-start | bytes 1179656 | tf_op jit(solution)/shard_map/ppermute | solution.py:14
  14.2 1.0 copy-start.2
  17.8 1.0 copy-start
  26.6 55.4 %all-to-all-start = ((f32[24,1,9216]{2,1,0:T(1,128)}), f32[24,1,9216]{2,1,0:T(1,128)S(1)}, u32[]{:S(2)}, u32[]{:S(2)}) async-start(f32[24,1,9216]{2,1,0:T(1,128)} %bitcast.185), calls=%async_computation | async-start | bytes 1769472 | tf_op jit(solution)/shard_map/all_to_all | solution.py:30
  55.5 49.6 %copy-start.1 = (bf16[1,64,1,8,128]{4,3,2,1,0:T(8,128)(2,1)S(1)}, bf16[1,64,1,8,128]{4,3,2,1,0:T(8,128)(2,1)}, u32[]{:S(2)}) copy-start(bf16[1,64,1,8,128]{4,3,2,1,0:T(8,128)(2,1)} %param.3) | copy-start | bytes 393220
  83.2 36.1 %all-to-all-start.1 = ((f32[32,1,288]{2,1,0:T(1,128)}), f32[32,1,288]{2,1,0:T(1,128)S(1)}, u32[]{:S(2)}, u32[]{:S(2)}) async-start(f32[32,1,288]{2,1,0:T(1,128)} %all_to_all.11), calls=%async_computation.1 | async-start | bytes 98304 | tf_op jit(solution)/shard_map/all_to_all | solution.py:30
where the time goes:
time: 120 us
  starting transfers between devices  54.7 us (46%)
  waiting for transfers between devices  44.2 us (37%)
  matrix products  12.7 us (11%)
  local copies, waits for them, and re-layouts  4.81 us (4%)
  other arithmetic  2.42 us (2%)
    all_to_all x2, starting transfers between devices, summed_on_arrival(): pieces = lax.all_to_all(split_up(x, dim, size), axis, 0, 0, tiled=True)  48 us
    all_to_all x2, waiting for transfers between devices, summed_on_arrival(): pieces = lax.all_to_all(split_up(x, dim, size), axis, 0, 0, tiled=True)  39.5 us
    dot_general x27, matrix products, on_device(): jnp.einsum('ic,scxyz->sixyz', weight[tap], window, preferred_element_type...  6.4 us
    dot_general x27, matrix products, on_device(): jnp.einsum('sixyz,scxyz->ic', moved, grad_out, preferred_element_type=jnp...  6.29 us
    ppermute x1, starting transfers between devices, padded(): lax.ppermute(lax.slice_in_dim(block, block.shape[dim] - width, None, axis...  5.47 us
    ppermute x1, waiting for transfers between devices, padded(): lax.ppermute(lax.slice_in_dim(block, 0, width, axis=dim), axis, backward)  3.2 us
    unnamed x8, local copies, waits for them, and re-layouts  3.01 us
  transfers between devices with their start and end apart: 4, of which 4 were waited for; matrix products, arithmetic and copies ran while one was open for 3% of the time, Pallas kernels for 0%

commit v1 on v0

v1 whole, which is shorter than its diff:
```python
import functools

import jax
import jax.numpy as jnp
from jax import lax
from jax.experimental import pallas as pl
from jax.experimental.pallas import tpu as pltpu
from jax.sharding import PartitionSpec as P

slope = 0.3
CIN, COUT, YC, ZC, TAPS = 64, 128, 8, 128, 27
ROWS = TAPS * CIN
TOP = 12.0


def shifted_lanes(tile, by):
    lane = lax.broadcasted_iota(jnp.int32, tile.shape, 1)
    if by > 0:
        return jnp.where(lane > 0, pltpu.roll(tile, 1, 1), 0.0)
    return jnp.where(lane < ZC - 1, pltpu.roll(tile, ZC - 1, 1), 0.0)


def kernel(factor, act_ref, own_ref, low_ref, high_ref, w_ref, gin_ref, wg_ref, exp_ref, wide, acts, grads, hids):
    for plane, (u, ref) in enumerate(((-1, high_ref), (0, own_ref), (1, low_ref))):
        wide[...] = ref[...].astype(jnp.float32).reshape(COUT * YC, ZC)
        for y in range(YC):
            tile = wide[pl.ds(y, COUT, stride=YC), :]
            for w in (-1, 0, 1):
                moved = tile if w == 0 else shifted_lanes(tile, w)
                row = (plane * 3 + w + 1) * COUT
                grads[row : row + COUT, y * ZC : (y + 1) * ZC] = moved.astype(jnp.bfloat16)
    act = act_ref[...].astype(jnp.float32)
    hidden = jnp.where(act > 0, act, slope * act).astype(jnp.bfloat16)
    acts[...] = hidden.astype(jnp.float32).reshape(CIN * YC, ZC)
    for y in range(YC):
        tile = acts[pl.ds(y, CIN, stride=YC), :].astype(jnp.bfloat16)
        for v in (-1, 0, 1):
            if 0 <= y - v < YC:
                hids[(v + 1) * CIN : (v + 2) * CIN, (y - v) * ZC : (y - v + 1) * ZC] = tile
    none = jnp.zeros((CIN, ZC), jnp.bfloat16)
    hids[0:CIN, 0:ZC] = none
    hids[2 * CIN : 3 * CIN, (YC - 1) * ZC : YC * ZC] = none

    taps = lax.dot_general(
        hids[...], grads[...], (((1,), (1,)), ((), ())), preferred_element_type=jnp.float32
    )
    most = jnp.max(jnp.abs(taps), keepdims=True) * factor
    exponent = jnp.floor(jnp.log2(jnp.maximum(most, 1e-36))) + 1.0
    exp_ref[...] = jnp.broadcast_to(exponent, exp_ref.shape)
    scale = jnp.broadcast_to(jnp.exp2(TOP - exponent) * factor, (CIN, COUT))
    for u in range(3):
        for v in range(3):
            for w in range(3):
                tap = 9 * u + 3 * v + w
                block = taps[v * CIN : (v + 1) * CIN, (u * 3 + w) * COUT : (u * 3 + w + 1) * COUT]
                wg_ref[tap * CIN : (tap + 1) * CIN, :] = (block * scale).astype(wg_ref.dtype)

    weights = jnp.concatenate(
        [
            jnp.concatenate([w_ref[9 * u + 3 * v + w] for u in range(3) for w in range(3)], axis=1)
            for v in range(3)
        ],
        axis=0,
    )
    sums = lax.dot_general(
        weights, grads[...], (((1,), (0,)), ((), ())), preferred_element_type=jnp.float32
    )
    for y in range(YC):
        total = sums[CIN : 2 * CIN, y * ZC : (y + 1) * ZC]
        if y + 1 < YC:
            total = total + sums[0:CIN, (y + 1) * ZC : (y + 2) * ZC]
        if y - 1 >= 0:
            total = total + sums[2 * CIN : 3 * CIN, (y - 1) * ZC : y * ZC]
        acts[pl.ds(y, CIN, stride=YC), :] = total
    grad_hidden = acts[...].reshape(CIN, YC, ZC)
    gin_ref[...] = (grad_hidden * jnp.where(act > 0, 1.0, slope)).astype(jnp.bfloat16)


def local_grads(factor, act, own, low, high, weight, wg_dtype):
    return pl.pallas_call(
        functools.partial(kernel, factor),
        out_shape=(
            jax.ShapeDtypeStruct((CIN, YC, ZC), jnp.bfloat16),
            jax.ShapeDtypeStruct((ROWS, COUT), wg_dtype),
            jax.ShapeDtypeStruct((8, 128), jnp.float32),
        ),
        in_specs=[pl.BlockSpec(memory_space=pltpu.VMEM)] * 5,
        out_specs=tuple([pl.BlockSpec(memory_space=pltpu.VMEM)] * 3),
        scratch_shapes=[
            pltpu.VMEM((COUT * YC, ZC), jnp.float32),
            pltpu.VMEM((CIN * YC, ZC), jnp.float32),
            pltpu.VMEM((9 * COUT, YC * ZC), jnp.bfloat16),
            pltpu.VMEM((3 * CIN, YC * ZC), jnp.bfloat16),
        ],
        compiler_params=pltpu.CompilerParams(vmem_limit_bytes=20 * 1024 * 1024),
        cost_estimate=pl.CostEstimate(flops=900_000_000, bytes_accessed=2_500_000, transcendentals=0),
        name="local_grads",
    )(act, own, low, high, weight)


XS, ZL, ZH, YS, CS = 4, 6, 2, 8, 2


def device(x, zl, zh, y, c):
    return (x * ZL + zl) * ZH * YS * CS + zh * YS * CS + y * CS + c


def groups():
    along_x = [[x * ZL + zl for x in range(XS)] for zl in range(ZL)]
    along_z = [
        [device(x, zl, zh, y, c) for zl in range(ZL) for zh in range(ZH)]
        for x in range(XS)
        for y in range(YS)
        for c in range(CS)
    ]
    along_y = [[zh * YS * CS + i for i in range(YS * CS)] for zh in range(ZH)]
    return along_x, along_z, along_y


def coded(scaled, exponent):
    mark = jnp.broadcast_to(exponent, (scaled.shape[0], 16, 128)).astype(jnp.float16)
    return jnp.concatenate([scaled.astype(jnp.float16), mark], axis=1)


def on_device(pre_act, grad_out, weight):
    count = pre_act.shape[0] * 32 * pre_act.shape[2] * 24 * YC * ZC
    factor = float(1.0 / count**0.5)
    steps = lax.axis_size("space")
    forward = [(i, i + 1) for i in range(steps - 1)]
    backward = [(i + 1, i) for i in range(steps - 1)]
    own = grad_out.reshape(COUT, YC, ZC)
    low = lax.ppermute(own, "space", forward)
    high = lax.ppermute(own, "space", backward)
    grad_in, partial, exponent = local_grads(
        factor, pre_act.reshape(CIN, YC, ZC), own, low, high, weight, jnp.float32
    )
    along_x, along_z, along_y = groups()
    rows = ROWS // XS
    sent = coded(partial.reshape(XS, rows, COUT), exponent[0, 0])
    got = lax.all_to_all(sent, "space", 0, 0, tiled=True, axis_index_groups=along_x)
    exps = got[:, rows, 0].astype(jnp.float32)
    largest = jnp.max(exps) + 2.0
    weights = jnp.exp2(exps - largest)
    part = jnp.sum(got[:, :rows].astype(jnp.float32) * weights[:, None, None], axis=0)
    rows = rows // (ZL * ZH)
    sent = coded(part.reshape(ZL * ZH, rows, COUT), largest)
    got = lax.all_to_all(sent, ("space", "batch"), 0, 0, tiled=True, axis_index_groups=along_z)
    weights = jnp.exp2(got[:, rows, 0].astype(jnp.float32) - TOP)
    part = jnp.sum(got[:, :rows].astype(jnp.float32) * weights[:, None, None], axis=0)
    sent = part.reshape(YS * CS, rows * COUT // (YS * CS))
    got = lax.all_to_all(sent, "batch", 0, 0, tiled=True, axis_index_groups=along_y)
    weight_grad = jnp.sum(got, axis=0)
    return (grad_in.reshape(pre_act.shape), weight_grad)


def solution(mesh):
    return jax.shard_map(
        on_device,
        mesh=mesh,
        in_specs=(
            P("batch", None, "space", None, None),
            P("batch", None, "space", None, None),
            P(),
        ),
        out_specs=(P("batch", None, "space", None, None), P(("space", "batch"))),
        check_vma=False,
    )
```

time: 120 us -> 86.5 us (0.72)
  blocking collectives: 0 us -> 65.7 us
  starting transfers between devices: 54.7 us -> 6.75 us
  waiting for transfers between devices: 44.2 us -> 3.6 us
  matrix products: 12.7 us -> 0 us
  Pallas kernels: 0 us -> 2.62 us
    all_to_all x0 -> x3, blocking collectives: none -> 65.7 us  [the longest x1 28 us: on_device(): lax.all_to_all(sent, 'space', 0, 0, tiled=True, axis_index_groups=along_x)]
    all_to_all x2 -> x0, starting transfers between devices: 48 us -> none  [summed_on_arrival(): pieces = lax.all_to_all(split_up(x, dim, size), axis, 0, 0, tiled=True)]
    all_to_all x2 -> x0, waiting for transfers between devices: 39.5 us -> none  [summed_on_arrival(): pieces = lax.all_to_all(split_up(x, dim, size), axis, 0, 0, tiled=True)]
    dot_general x54 -> x0, matrix products: 12.7 us -> none  [the longest x27 6.4 us: on_device(): jnp.einsum('ic,scxyz->sixyz', weight[tap], window, preferred_element_type...]
    pallas_call x0 -> x1, Pallas kernels: none -> 2.62 us  [local_grads(): pl.pallas_call(functools.partial(kernel, factor), out_shape=(jax.ShapeDty...]
    unnamed x8 -> x7, local copies, waits for them, and re-layouts: 3.01 us -> 2.97 us
  transfers between devices with their start and end apart: 4 -> 2, of which waited for: 4 -> 2; matrix products, arithmetic and copies ran while one was open for 3% -> 0% of each run, Pallas kernels for 0% -> 0%
where the time goes in v1:
time: 86.5 us; the launch traced here: 86.1 us
  blocking collectives  65.7 us (76%)
  starting transfers between devices  6.75 us (8%)
  local copies, waits for them, and re-layouts  4.41 us (5%)
  waiting for transfers between devices  3.6 us (4%)
  Pallas kernels  2.62 us (3%)
  other arithmetic  1.71 us (2%)
  between operations  1.37 us (2%)
    all_to_all x1, blocking collectives, on_device(): lax.all_to_all(sent, 'space', 0, 0, tiled=True, axis_index_groups=along_x)  28 us
    all_to_all x1, blocking collectives, on_device(): lax.all_to_all(sent, 'batch', 0, 0, tiled=True, axis_index_groups=along_y)  19 us
    all_to_all x1, blocking collectives, on_device(): lax.all_to_all(sent, ('space', 'batch'), 0, 0, tiled=True, axis_index_gro...  18.6 us
    ppermute x1, starting transfers between devices, on_device(): low = lax.ppermute(own, 'space', forward)  5.46 us
    unnamed x7, local copies, waits for them, and re-layouts  2.97 us
    pallas_call x1, Pallas kernels, local_grads(): pl.pallas_call(functools.partial(kernel, factor), out_shape=(jax.ShapeDty...  2.62 us
    ppermute x1, waiting for transfers between devices, on_device(): high = lax.ppermute(own, 'space', backward)  2.02 us
  transfers between devices with their start and end apart: 2, of which 2 were waited for; matrix products, arithmetic and copies ran while one was open for 0% of the time, Pallas kernels for 0%

profile of v1, /device:TPU:1, one launch (start us, length us, event | category | flops | bytes accessed | tf_op | source)
XLA Modules:
  0.0 86.1 jit_solution(4203559793671040318)
XLA Ops:
  0.6 1.3 %collective-permute-start.1 = (bf16[128,8,128]{2,1,0:T(8,128)(2,1)}, bf16[128,8,128]{2,1,0:T(8,128)(2,1)S(1)}, u32[]{:S(2)}, u32[]{:S(2)}) collective-permute-start(bf16[128,8,128]{2,1,0:T(8,128)(2,1)} %bitcast.9), channel_id=1, source_target_pairs={{32,0},{64,32},{96,64},{128,96},{160,128},{192,160},{224,192},{256... | collective-permute-start | bytes 786440 | tf_op jit(solution)/shard_map/ppermute | solution.py:133
  1.9 5.5 %collective-permute-start = (bf16[128,8,128]{2,1,0:T(8,128)(2,1)}, bf16[128,8,128]{2,1,0:T(8,128)(2,1)S(1)}, u32[]{:S(2)}, u32[]{:S(2)}) collective-permute-start(bf16[128,8,128]{2,1,0:T(8,128)(2,1)} %bitcast.10), channel_id=1, source_target_pairs={{0,32},{32,64},{64,96},{96,128},{128,160},{160,192},{192,224},{224... | collective-permute-start | bytes 786440 | tf_op jit(solution)/shard_map/ppermute | solution.py:132
  7.4 2.0 %collective-permute-done.1.high_ref = bf16[128,8,128]{2,1,0:T(8,128)(2,1)S(1)} collective-permute-done((bf16[128,8,128]{2,1,0:T(8,128)(2,1)}, bf16[128,8,128]{2,1,0:T(8,128)(2,1)S(1)}, u32[]{:S(2)}, u32[]{:S(2)}) %collective-permute-start.1) | collective-permute-done | bytes 262176 | tf_op jit(solution)/shard_map/ppermute | solution.py:133
  9.4 1.6 %collective-permute-done.low_ref = bf16[128,8,128]{2,1,0:T(8,128)(2,1)S(1)} collective-permute-done((bf16[128,8,128]{2,1,0:T(8,128)(2,1)}, bf16[128,8,128]{2,1,0:T(8,128)(2,1)S(1)}, u32[]{:S(2)}, u32[]{:S(2)}) %collective-permute-start) | collective-permute-done | bytes 262176 | tf_op jit(solution)/shard_map/ppermute | solution.py:132
  11.0 0.0 copy-start
  11.0 1.0 %copy-done = bf16[27,64,128]{2,1,0:T(8,128)(2,1)S(1)} copy-done((bf16[27,64,128]{2,1,0:T(8,128)(2,1)S(1)}, bf16[27,64,128]{2,1,0:T(8,128)(2,1)}, u32[]{:S(2)}) %copy-start) | copy-done | bytes 442392
  12.0 0.0 copy-start.1
  12.0 0.9 %copy-done.1 = bf16[1,128,1,8,128]{4,3,2,1,0:T(8,128)(2,1)S(1)} copy-done((bf16[1,128,1,8,128]{4,3,2,1,0:T(8,128)(2,1)S(1)}, bf16[1,128,1,8,128]{4,3,2,1,0:T(8,128)(2,1)}, u32[]{:S(2)}) %copy-start.1) | copy-done | bytes 262168
  13.0 0.0 copy-start.2
  13.0 0.9 %copy-done.2 = bf16[1,64,1,8,128]{4,3,2,1,0:T(8,128)(2,1)S(1)} copy-done((bf16[1,64,1,8,128]{4,3,2,1,0:T(8,128)(2,1)S(1)}, bf16[1,64,1,8,128]{4,3,2,1,0:T(8,128)(2,1)}, u32[]{:S(2)}) %copy-start.2) | copy-done | bytes 131096
  13.9 2.6 %local_grads.1 = (bf16[64,8,128]{2,1,0:T(8,128)(2,1)}, f32[1728,128]{1,0:T(8,128)S(1)}, f32[8,128]{1,0:T(8,128)S(1)}) custom-call(bf16[64,8,128]{2,1,0:T(8,128)(2,1)S(1)} %bitcast.12, bf16[128,8,128]{2,1,0:T(8,128)(2,1)S(1)} %bitcast.11, bf16[128,8,128]{2,1,0:T(8,128)(2,1)S(1)} %collective-permute-done.low_ref, ...), custom_call_target="tpu_custom_call" | custom-call | flops 900000000 | bytes 2500000 | tf_op jit(solution)/shard_map/local_grads/pallas_call | solution.py:80
  16.5 0.5 slice.16
  17.0 0.1 convert_element_type.36
  17.1 0.7 concatenate.6
  17.8 28.0 %all_to_all.19 = f16[4,448,128]{2,1,0:T(8,128)(2,1)S(1)} all-to-all(f16[4,448,128]{2,1,0:T(8,128)(2,1)S(1)} %concatenate.6), channel_id=1, replica_groups={{0,192,384,576},{32,224,416,608},{64,256,448,640},{96,288,480,672},{128..., dimensions={0} | all-to-all | bytes 917504 | tf_op jit(solution)/shard_map/all_to_all | solution.py:140
  45.8 0.6 fusion
  47.1 0.1 exponential_reduce_fusion
  47.2 0.2 multiply_reduce_fusion
  47.5 18.6 %all_to_all.20 = f16[12,52,128]{2,1,0:T(8,128)(2,1)S(1)} all-to-all(f16[12,52,128]{2,1,0:T(8,128)(2,1)S(1)} %concatenate.7), channel_id=1, replica_groups={{0,16,32,48,64,80,96,112,128,144,160,176},{1,17,33,49,65,81,97,113,129,..., dimensions={0} | all-to-all | bytes 319488 | tf_op jit(solution)/shard_map/all_to_all | solution.py:147
  66.2 0.1 copy.17
  66.3 0.1 multiply_reduce_fusion.1
  66.4 0.1 all_to_all.14
  66.5 19.0 %all_to_all.21 = f32[16,1,288]{2,1,0:T(1,128)S(1)} all-to-all(f32[16,1,288]{2,1,0:T(1,128)S(1)} %all_to_all.14), channel_id=1, replica_groups={{0,1,2,3,4,5,6,7,8,9,10,11,12,13,14,15},{16,17,18,19,20,21,22,23,24,25,..., dimensions={0} | all-to-all | bytes 36864 | tf_op jit(solution)/shard_map/all_to_all | solution.py:151
  85.5 0.6 reduce_sum.29
  (6 shorter events, 0.1 us)
Async XLA Ops:
  0.6 8.8 %collective-permute-start.1 = (bf16[128,8,128]{2,1,0:T(8,128)(2,1)}, bf16[128,8,128]{2,1,0:T(8,128)(2,1)S(1)}, u32[]{:S(2)}, u32[]{:S(2)}) collective-permute-start(bf16[128,8,128]{2,1,0:T(8,128)(2,1)} %bitcast.9), channel_id=1, source_target_pairs={{32,0},{64,32},{96,64},{128,96},{160,128},{192,160},{224,192},{256... | collective-permute-start | bytes 786440 | tf_op jit(solution)/shard_map/ppermute | solution.py:133
  1.9 9.1 %collective-permute-start = (bf16[128,8,128]{2,1,0:T(8,128)(2,1)}, bf16[128,8,128]{2,1,0:T(8,128)(2,1)S(1)}, u32[]{:S(2)}, u32[]{:S(2)}) collective-permute-start(bf16[128,8,128]{2,1,0:T(8,128)(2,1)} %bitcast.10), channel_id=1, source_target_pairs={{0,32},{32,64},{64,96},{96,128},{128,160},{160,192},{192,224},{224... | collective-permute-start | bytes 786440 | tf_op jit(solution)/shard_map/ppermute | solution.py:132
  11.0 1.0 %copy-start = (bf16[27,64,128]{2,1,0:T(8,128)(2,1)S(1)}, bf16[27,64,128]{2,1,0:T(8,128)(2,1)}, u32[]{:S(2)}) copy-start(bf16[27,64,128]{2,1,0:T(8,128)(2,1)} %w_ref.1) | copy-start | bytes 1327108
  12.0 0.9 %copy-start.1 = (bf16[1,128,1,8,128]{4,3,2,1,0:T(8,128)(2,1)S(1)}, bf16[1,128,1,8,128]{4,3,2,1,0:T(8,128)(2,1)}, u32[]{:S(2)}) copy-start(bf16[1,128,1,8,128]{4,3,2,1,0:T(8,128)(2,1)} %param.4) | copy-start | bytes 786436
  13.0 0.9 %copy-start.2 = (bf16[1,64,1,8,128]{4,3,2,1,0:T(8,128)(2,1)S(1)}, bf16[1,64,1,8,128]{4,3,2,1,0:T(8,128)(2,1)}, u32[]{:S(2)}) copy-start(bf16[1,64,1,8,128]{4,3,2,1,0:T(8,128)(2,1)} %param.3) | copy-start | bytes 393220

commit v2 on v1

v2 whole, which is shorter than its diff:
```python
import functools

import jax
import jax.numpy as jnp
from jax import lax
from jax.experimental import pallas as pl
from jax.experimental.pallas import tpu as pltpu
from jax.sharding import PartitionSpec as P

slope = 0.3
CIN, COUT, YC, ZC, TAPS = 64, 128, 8, 128, 27
CELLS = YC * ZC
ROWS = TAPS * CIN
XS, ZL, ZH, YS, CS = 4, 6, 2, 8, 2
ZS, YCS = ZL * ZH, YS * CS
XROWS = ROWS // XS
ZROWS = XROWS // ZS
PART = 3
MARKS = 16
TOP = 12.0


def shifted_lanes(tile, by):
    lane = lax.broadcasted_iota(jnp.int32, tile.shape, 1)
    if by > 0:
        return jnp.where(lane > 0, pltpu.roll(tile, 1, 1), 0.0)
    return jnp.where(lane < ZC - 1, pltpu.roll(tile, ZC - 1, 1), 0.0)


def spread(ref, wide, grads, first):
    wide[...] = ref[...].astype(jnp.float32).reshape(COUT * YC, ZC)
    for y in range(YC):
        tile = wide[pl.ds(y, COUT, stride=YC), :]
        for w in (-1, 0, 1):
            moved = tile if w == 0 else shifted_lanes(tile, w)
            row = first + (w + 1) * COUT
            grads[row : row + COUT, y * ZC : (y + 1) * ZC] = moved.astype(jnp.bfloat16)


def by_taps(hids, grads):
    return lax.dot_general(
        hids[...], grads[...], (((1,), (1,)), ((), ())), preferred_element_type=jnp.float32
    )


def by_cells(weights, grads):
    return lax.dot_general(
        weights[...], grads[...], (((1,), (0,)), ((), ())), preferred_element_type=jnp.float32
    )


def own_kernel(act_ref, own_ref, w_ref, hid_ref, tap_ref, sum_ref, side_ref, wide, acts, grads, mids):
    spread(own_ref, wide, grads, 0)
    act = act_ref[...].astype(jnp.float32)
    hidden = jnp.where(act > 0, act, slope * act).astype(jnp.bfloat16)
    acts[...] = hidden.astype(jnp.float32).reshape(CIN * YC, ZC)
    for y in range(YC):
        tile = acts[pl.ds(y, CIN, stride=YC), :].astype(jnp.bfloat16)
        for v in (-1, 0, 1):
            if 0 <= y - v < YC:
                hid_ref[(v + 1) * CIN : (v + 2) * CIN, (y - v) * ZC : (y - v + 1) * ZC] = tile
    none = jnp.zeros((CIN, ZC), jnp.bfloat16)
    hid_ref[0:CIN, 0:ZC] = none
    hid_ref[2 * CIN : 3 * CIN, (YC - 1) * ZC : YC * ZC] = none
    for v in range(3):
        for w in range(3):
            rows, lanes = slice(v * CIN, (v + 1) * CIN), slice(w * COUT, (w + 1) * COUT)
            mids[rows, lanes] = w_ref[9 + 3 * v + w]
            side_ref[rows, lanes] = w_ref[3 * v + w]
            side_ref[rows, (w + 3) * COUT : (w + 4) * COUT] = w_ref[18 + 3 * v + w]
    tap_ref[...] = by_taps(hid_ref, grads)
    sum_ref[...] = by_cells(mids, grads)


def side_kernel(
    factor, act_ref, low_ref, high_ref, hid_ref, tap_ref, sum_ref, side_ref, sent_ref, gin_ref, wide, acts, grads
):
    spread(high_ref, wide, grads, 0)
    spread(low_ref, wide, grads, 3 * COUT)
    outer = by_taps(hid_ref, grads)
    inner = tap_ref[...]
    most = jnp.maximum(
        jnp.max(jnp.abs(outer), keepdims=True), jnp.max(jnp.abs(inner), keepdims=True)
    )
    exponent = jnp.floor(jnp.log2(jnp.maximum(most * factor, 1e-30))) + 1.0
    scale = jnp.broadcast_to(jnp.exp2(TOP - exponent) * factor, (CIN, COUT))
    for x in range(XS):
        sent_ref[x, XROWS : XROWS + MARKS, :] = jnp.broadcast_to(exponent, (MARKS, COUT))
    for tap in range(TAPS):
        u, v, w = tap // 9, tap // 3 % 3, tap % 3
        rows = slice(v * CIN, (v + 1) * CIN)
        if u == 1:
            block = inner[rows, w * COUT : (w + 1) * COUT]
        else:
            lane = (u // 2 * 3 + w) * COUT
            block = outer[rows, lane : lane + COUT]
        block = block * scale
        first = tap * CIN
        while first < (tap + 1) * CIN:
            x = first // XROWS
            last = min((tap + 1) * CIN, (x + 1) * XROWS)
            sent_ref[x, first - x * XROWS : last - x * XROWS, :] = block[first - tap * CIN : last - tap * CIN]
            first = last
    sums = by_cells(side_ref, grads) + sum_ref[...]
    for y in range(YC):
        total = sums[CIN : 2 * CIN, y * ZC : (y + 1) * ZC]
        if y + 1 < YC:
            total = total + sums[0:CIN, (y + 1) * ZC : (y + 2) * ZC]
        if y - 1 >= 0:
            total = total + sums[2 * CIN : 3 * CIN, (y - 1) * ZC : y * ZC]
        acts[pl.ds(y, CIN, stride=YC), :] = total
    grad_hidden = acts[...].reshape(CIN, YC, ZC)
    act = act_ref[...].astype(jnp.float32)
    gin_ref[...] = (grad_hidden * jnp.where(act > 0, 1.0, slope)).astype(jnp.bfloat16)


def after_x_kernel(got_ref, sent_ref, total):
    exps = [got_ref[i, XROWS : XROWS + 1, :] for i in range(XS)]
    largest = functools.reduce(jnp.maximum, exps) + 2.0
    total[...] = sum(got_ref[i, 0:XROWS, :] * jnp.exp2(exps[i] - largest) for i in range(XS))
    for part in range(YCS):
        row = 9 * (part // 4) + 2 * (part % 4)
        for i in range(PART):
            sent_ref[part, i * ZS : (i + 1) * ZS, :] = total[pl.ds(row + i, ZS, stride=ZROWS), :]
        sent_ref[part, PART * ZS : PART * ZS + 12, :] = jnp.broadcast_to(largest, (12, COUT))


def after_y_kernel(got_ref, sent_ref):
    total = jnp.zeros((PART * ZS, COUT), jnp.float32)
    for i in range(YCS):
        weight = jnp.exp2(got_ref[i, PART * ZS : PART * ZS + 1, :] - TOP)
        total = total + got_ref[i, 0 : PART * ZS, :] * weight
    for i in range(PART):
        sent_ref[:, i, :] = total[i * ZS : (i + 1) * ZS]


def call(body, name, outs, scratch, flops, *args):
    vmem = pl.BlockSpec(memory_space=pltpu.VMEM)
    return pl.pallas_call(
        body,
        out_shape=tuple(jax.ShapeDtypeStruct(shape, dtype) for shape, dtype in outs),
        in_specs=[vmem] * len(args),
        out_specs=tuple([vmem] * len(outs)),
        scratch_shapes=[pltpu.VMEM(shape, dtype) for shape, dtype in scratch],
        compiler_params=pltpu.CompilerParams(vmem_limit_bytes=16 * 1024 * 1024),
        cost_estimate=pl.CostEstimate(flops=flops, bytes_accessed=2_000_000, transcendentals=0),
        name=name,
    )(*args)


def device(x, zl, zh, y, c):
    return (x * ZL + zl) * ZH * YCS + zh * YCS + y * CS + c


def groups():
    along_x = [[x * ZL + zl for x in range(XS)] for zl in range(ZL)]
    along_y = [[zh * YCS + i for i in range(YCS)] for zh in range(ZH)]
    along_z = [
        [device(x, zl, zh, y, c) for zl in range(ZL) for zh in range(ZH)]
        for x in range(XS)
        for y in range(YS)
        for c in range(CS)
    ]
    return along_x, along_y, along_z


def exchanged(x, axis, members):
    return lax.all_to_all(x, axis, 0, 0, tiled=True, axis_index_groups=members)


def on_device(pre_act, grad_out, weight):
    f32, bf16, f16 = jnp.float32, jnp.bfloat16, jnp.float16
    count = pre_act.shape[0] * lax.axis_size("batch") * lax.axis_size("space") * CELLS
    factor = float(1.0 / count**0.5)
    steps = lax.axis_size("space")
    forward = [(i, i + 1) for i in range(steps - 1)]
    backward = [(i + 1, i) for i in range(steps - 1)]
    along_x, along_y, along_z = groups()

    act = pre_act.reshape(CIN, YC, ZC)
    own = grad_out.reshape(COUT, YC, ZC)
    low = lax.ppermute(own, "space", forward)
    high = lax.ppermute(own, "space", backward)
    plane = ((COUT * YC, ZC), f32)
    small = ((CIN * YC, ZC), f32)
    hids, taps, sums, sides = call(
        own_kernel,
        "own_plane",
        [((3 * CIN, CELLS), bf16), ((3 * CIN, 3 * COUT), f32), ((3 * CIN, CELLS), f32), ((3 * CIN, 6 * COUT), bf16)],
        [plane, small, ((3 * COUT, CELLS), bf16), ((3 * CIN, 3 * COUT), bf16)],
        1_000_000_000,
        act, own, weight,
    )
    sent, grad_in = call(
        functools.partial(side_kernel, factor),
        "side_planes",
        [((XS, XROWS + MARKS, COUT), f32), ((CIN, YC, ZC), bf16)],
        [plane, small, ((6 * COUT, CELLS), bf16)],
        2_000_000_000,
        act, low, high, hids, taps, sums, sides,
    )
    got = exchanged(sent.astype(f16), "space", along_x).astype(f32)
    (sent,) = call(
        after_x_kernel, "after_x", [((YCS, PART * ZS + 12, COUT), f32)], [((XROWS, COUT), f32)], 1_000_000, got
    )
    got = exchanged(sent.astype(f16), "batch", along_y).astype(f32)
    (sent,) = call(after_y_kernel, "after_y", [((ZS, PART, COUT), f32)], [], 1_000_000, got)
    got = exchanged(sent, ("space", "batch"), along_z)
    total = jnp.sum(got, axis=0).reshape(-1)
    start = (lax.axis_index("batch") & 3) * 32
    weight_grad = lax.dynamic_slice(total, (start,), (ROWS * COUT // 768,))
    return (grad_in.reshape(pre_act.shape), weight_grad)


def solution(mesh):
    return jax.shard_map(
        on_device,
        mesh=mesh,
        in_specs=(
            P("batch", None, "space", None, None),
            P("batch", None, "space", None, None),
            P(),
        ),
        out_specs=(P("batch", None, "space", None, None), P(("space", "batch"))),
        check_vma=False,
    )
```

time: 86.5 us -> 79.9 us (0.924)
  blocking collectives: 65.7 us -> 38.3 us
  starting transfers between devices: 6.75 us -> 21.2 us
  waiting for transfers between devices: 3.6 us -> 11.9 us
  other arithmetic: 1.71 us -> 0.2 us
  Pallas kernels: 2.62 us -> 3.61 us
  local copies, waits for them, and re-layouts: 4.41 us -> 3.51 us
    all_to_all x3 -> x2, blocking collectives: 65.7 us -> 38.3 us  [exchanged(): return lax.all_to_all(x, axis, 0, 0, tiled=True, axis_index_groups=members)]
    all_to_all x0 -> x1, starting transfers between devices: none -> 15.1 us  [exchanged(): return lax.all_to_all(x, axis, 0, 0, tiled=True, axis_index_groups=members)]
    all_to_all x0 -> x1, waiting for transfers between devices: none -> 8.97 us  [exchanged(): return lax.all_to_all(x, axis, 0, 0, tiled=True, axis_index_groups=members)]
    ppermute x1, waiting for transfers between devices: 1.58 us -> 0.01 us  [on_device(): low = lax.ppermute(own, 'space', forward)]
    pallas_call x1 -> x4, Pallas kernels: 2.62 us -> 3.61 us  [call(): pl.pallas_call(body, out_shape=tuple((jax.ShapeDtypeStruct(shape, dtype)...]
    ppermute x1, waiting for transfers between devices: 2.02 us -> 2.92 us  [on_device(): high = lax.ppermute(own, 'space', backward)]
    reduce_sum x3 -> x1, other arithmetic: 0.89 us -> 0.02 us  [on_device(): total = jnp.sum(got, axis=0).reshape(-1)]
    unnamed x7 -> x6, local copies, waits for them, and re-layouts: 2.97 us -> 2.86 us
  transfers between devices with their start and end apart: 2 -> 3, of which waited for: 2 -> 2; matrix products, arithmetic and copies ran while one was open for 0% -> 0% of each run, Pallas kernels for 0% -> 1%
where the time goes in v2:
time: 79.9 us; the launch traced here: 79.5 us
  blocking collectives  38.3 us (48%)
  starting transfers between devices  21.2 us (27%)
  waiting for transfers between devices  11.9 us (15%)
  Pallas kernels  3.61 us (5%)
  local copies, waits for them, and re-layouts  3.51 us (4%)
    all_to_all x2, blocking collectives, exchanged(): return lax.all_to_all(x, axis, 0, 0, tiled=True, axis_index_groups=members)  38.3 us
    all_to_all x1, starting transfers between devices, exchanged(): return lax.all_to_all(x, axis, 0, 0, tiled=True, axis_index_groups=members)  15.1 us
    all_to_all x1, waiting for transfers between devices, exchanged(): return lax.all_to_all(x, axis, 0, 0, tiled=True, axis_index_groups=members)  8.97 us
    ppermute x1, starting transfers between devices, on_device(): low = lax.ppermute(own, 'space', forward)  4.83 us
    pallas_call x4, Pallas kernels, call(): pl.pallas_call(body, out_shape=tuple((jax.ShapeDtypeStruct(shape, dtype)...  3.61 us
    ppermute x1, waiting for transfers between devices, on_device(): high = lax.ppermute(own, 'space', backward)  2.92 us
    unnamed x6, local copies, waits for them, and re-layouts  2.86 us
  transfers between devices with their start and end apart: 3, of which 2 were waited for; matrix products, arithmetic and copies ran while one was open for 0% of the time, Pallas kernels for 1%

profile of v2, /device:TPU:1, one launch (start us, length us, event | category | flops | bytes accessed | tf_op | source)
XLA Modules:
  0.0 79.5 jit_solution(5031817717361936705)
XLA Ops:
  0.6 4.8 %collective-permute-start = (bf16[128,8,128]{2,1,0:T(8,128)(2,1)}, bf16[128,8,128]{2,1,0:T(8,128)(2,1)S(1)}, u32[]{:S(2)}, u32[]{:S(2)}) collective-permute-start(bf16[128,8,128]{2,1,0:T(8,128)(2,1)} %bitcast.6), channel_id=1, source_target_pairs={{0,32},{32,64},{64,96},{96,128},{128,160},{160,192},{192,224},{224... | collective-permute-start | bytes 786440 | tf_op jit(solution)/shard_map/ppermute | solution.py:182
  5.5 1.3 %collective-permute-start.1 = (bf16[128,8,128]{2,1,0:T(8,128)(2,1)}, bf16[128,8,128]{2,1,0:T(8,128)(2,1)S(1)}, u32[]{:S(2)}, u32[]{:S(2)}) collective-permute-start(bf16[128,8,128]{2,1,0:T(8,128)(2,1)} %bitcast.7), channel_id=1, source_target_pairs={{32,0},{64,32},{96,64},{128,96},{160,128},{192,160},{224,192},{256... | collective-permute-start | bytes 786440 | tf_op jit(solution)/shard_map/ppermute | solution.py:183
  6.8 0.0 copy-start
  6.8 1.0 %copy-done = bf16[27,64,128]{2,1,0:T(8,128)(2,1)S(1)} copy-done((bf16[27,64,128]{2,1,0:T(8,128)(2,1)S(1)}, bf16[27,64,128]{2,1,0:T(8,128)(2,1)}, u32[]{:S(2)}) %copy-start) | copy-done | bytes 442392
  7.8 0.0 copy-start.1
  7.8 0.9 %copy-done.1 = bf16[1,128,1,8,128]{4,3,2,1,0:T(8,128)(2,1)S(1)} copy-done((bf16[1,128,1,8,128]{4,3,2,1,0:T(8,128)(2,1)S(1)}, bf16[1,128,1,8,128]{4,3,2,1,0:T(8,128)(2,1)}, u32[]{:S(2)}) %copy-start.1) | copy-done | bytes 262168
  8.7 0.0 copy-start.2
  8.7 0.9 %copy-done.2 = bf16[1,64,1,8,128]{4,3,2,1,0:T(8,128)(2,1)S(1)} copy-done((bf16[1,64,1,8,128]{4,3,2,1,0:T(8,128)(2,1)S(1)}, bf16[1,64,1,8,128]{4,3,2,1,0:T(8,128)(2,1)}, u32[]{:S(2)}) %copy-start.2) | copy-done | bytes 131096
  9.6 0.9 %own_plane.1 = (bf16[192,1024]{1,0:T(8,128)(2,1)S(1)}, f32[192,384]{1,0:T(8,128)S(1)}, f32[192,1024]{1,0:T(8,128)S(1)}, bf16[192,768]{1,0:T(8,128)(2,1)S(1)}) custom-call(bf16[64,8,128]{2,1,0:T(8,128)(2,1)S(1)} %bitcast.9, bf16[128,8,128]{2,1,0:T(8,128)(2,1)S(1)} %bitcast.8, bf16[27,64,128]{2,1,0:T(8,128)(2,1)S(1)} %copy-done), custom_call_target="tpu_custom_call" | custom-call | flops 1000000000 | bytes 2000000 | tf_op jit(solution)/shard_map/own_plane/pallas_call | solution.py:139
  10.5 0.0 collective-permute-done.low_ref
  10.5 2.9 %collective-permute-done.1.high_ref = bf16[128,8,128]{2,1,0:T(8,128)(2,1)S(1)} collective-permute-done((bf16[128,8,128]{2,1,0:T(8,128)(2,1)}, bf16[128,8,128]{2,1,0:T(8,128)(2,1)S(1)}, u32[]{:S(2)}, u32[]{:S(2)}) %collective-permute-start.1) | collective-permute-done | bytes 262176 | tf_op jit(solution)/shard_map/ppermute | solution.py:183
  13.4 2.0 %side_planes.1 = (f32[4,448,128]{2,1,0:T(8,128)S(1)}, bf16[64,8,128]{2,1,0:T(8,128)(2,1)}) custom-call(bf16[64,8,128]{2,1,0:T(8,128)(2,1)S(1)} %bitcast.10, bf16[128,8,128]{2,1,0:T(8,128)(2,1)S(1)} %collective-permute-done.low_ref, bf16[128,8,128]{2,1,0:T(8,128)(2,1)S(1)} %collective-permute-done.1.high_ref, bf16[192,1024]{1,0:T(8,128)(2,1)S(1)} %get-tuple-element.8.hid_ref, ...), custom_call_target="tpu_custom_call" | custom-call | flops 2000000000 | bytes 2000000 | tf_op jit(solution)/shard_map/side_planes/pallas_call | solution.py:139
  15.4 0.1 convert_element_type.12
  15.4 18.3 %all_to_all.15 = f16[4,448,128]{2,1,0:T(8,128)(2,1)S(1)} all-to-all(f16[4,448,128]{2,1,0:T(8,128)(2,1)S(1)} %convert_element_type.12), channel_id=1, replica_groups={{0,192,384,576},{32,224,416,608},{64,256,448,640},{96,288,480,672},{128..., dimensions={0} | all-to-all | bytes 917504 | tf_op jit(solution)/shard_map/all_to_all | solution.py:168
  33.7 0.1 convert_element_type.13.got_ref
  33.8 0.1 after_x.1
  34.0 20.1 %all_to_all.16 = f16[16,48,128]{2,1,0:T(8,128)(2,1)S(1)} all-to-all(f16[16,48,128]{2,1,0:T(8,128)(2,1)S(1)} %convert_element_type.14), channel_id=1, replica_groups={{0,1,2,3,4,5,6,7,8,9,10,11,12,13,14,15},{16,17,18,19,20,21,22,23,24,25,..., dimensions={0} | all-to-all | bytes 393216 | tf_op jit(solution)/shard_map/all_to_all | solution.py:168
  54.1 0.7 after_y.1
  54.7 15.1 %all-to-all-start.2 = ((f32[12,3,128]{2,1,0:T(4,128)}), f32[12,3,128]{2,1,0:T(4,128)S(1)}, u32[]{:S(2)}, u32[]{:S(2)}) async-start(f32[12,3,128]{2,1,0:T(4,128)} %after_y.1), calls=%async_computation.2 | async-start | bytes 49152 | tf_op jit(solution)/shard_map/all_to_all | solution.py:168
  69.9 9.0 %all-to-all-done.2 = f32[12,3,128]{2,1,0:T(4,128)S(1)} async-done(((f32[12,3,128]{2,1,0:T(4,128)}), f32[12,3,128]{2,1,0:T(4,128)S(1)}, u32[]{:S(2)}, u32[]{:S(2)}) %all-to-all-start.2) | async-done | bytes 18464 | tf_op jit(solution)/shard_map/all_to_all | solution.py:168
  78.8 0.7 dynamic_slice.3
  (3 shorter events, 0.1 us)
Async XLA Ops:
  0.6 9.9 %collective-permute-start = (bf16[128,8,128]{2,1,0:T(8,128)(2,1)}, bf16[128,8,128]{2,1,0:T(8,128)(2,1)S(1)}, u32[]{:S(2)}, u32[]{:S(2)}) collective-permute-start(bf16[128,8,128]{2,1,0:T(8,128)(2,1)} %bitcast.6), channel_id=1, source_target_pairs={{0,32},{32,64},{64,96},{96,128},{128,160},{160,192},{192,224},{224... | collective-permute-start | bytes 786440 | tf_op jit(solution)/shard_map/ppermute | solution.py:182
  5.5 8.0 %collective-permute-start.1 = (bf16[128,8,128]{2,1,0:T(8,128)(2,1)}, bf16[128,8,128]{2,1,0:T(8,128)(2,1)S(1)}, u32[]{:S(2)}, u32[]{:S(2)}) collective-permute-start(bf16[128,8,128]{2,1,0:T(8,128)(2,1)} %bitcast.7), channel_id=1, source_target_pairs={{32,0},{64,32},{96,64},{128,96},{160,128},{192,160},{224,192},{256... | collective-permute-start | bytes 786440 | tf_op jit(solution)/shard_map/ppermute | solution.py:183
  6.8 1.0 %copy-start = (bf16[27,64,128]{2,1,0:T(8,128)(2,1)S(1)}, bf16[27,64,128]{2,1,0:T(8,128)(2,1)}, u32[]{:S(2)}) copy-start(bf16[27,64,128]{2,1,0:T(8,128)(2,1)} %w_ref.1) | copy-start | bytes 1327108
  7.8 0.9 %copy-start.1 = (bf16[1,128,1,8,128]{4,3,2,1,0:T(8,128)(2,1)S(1)}, bf16[1,128,1,8,128]{4,3,2,1,0:T(8,128)(2,1)}, u32[]{:S(2)}) copy-start(bf16[1,128,1,8,128]{4,3,2,1,0:T(8,128)(2,1)} %param.4) | copy-start | bytes 786436
  8.7 0.9 %copy-start.2 = (bf16[1,64,1,8,128]{4,3,2,1,0:T(8,128)(2,1)S(1)}, bf16[1,64,1,8,128]{4,3,2,1,0:T(8,128)(2,1)}, u32[]{:S(2)}) copy-start(bf16[1,64,1,8,128]{4,3,2,1,0:T(8,128)(2,1)} %param.3) | copy-start | bytes 393220
  54.7 24.1 %all-to-all-start.2 = ((f32[12,3,128]{2,1,0:T(4,128)}), f32[12,3,128]{2,1,0:T(4,128)S(1)}, u32[]{:S(2)}, u32[]{:S(2)}) async-start(f32[12,3,128]{2,1,0:T(4,128)} %after_y.1), calls=%async_computation.2 | async-start | bytes 49152 | tf_op jit(solution)/shard_map/all_to_all | solution.py:168

commit v3 on v2

--- a/solution.py
+++ b/solution.py
@@ -16,7 +16,7 @@
 XROWS = ROWS // XS
 ZROWS = XROWS // ZS
 PART = 3
-MARKS = 16
+XMARKS, YMARKS = 8, 4
 TOP = 12.0
 
 
@@ -49,59 +49,59 @@
     )
 
 
-def own_kernel(act_ref, own_ref, w_ref, hid_ref, tap_ref, sum_ref, side_ref, wide, acts, grads, mids):
-    spread(own_ref, wide, grads, 0)
-    act = act_ref[...].astype(jnp.float32)
+def stack_hidden(act, acts, hids):
     hidden = jnp.where(act > 0, act, slope * act).astype(jnp.bfloat16)
     acts[...] = hidden.astype(jnp.float32).reshape(CIN * YC, ZC)
     for y in range(YC):
         tile = acts[pl.ds(y, CIN, stride=YC), :].astype(jnp.bfloat16)
         for v in (-1, 0, 1):
             if 0 <= y - v < YC:
-                hid_ref[(v + 1) * CIN : (v + 2) * CIN, (y - v) * ZC : (y - v + 1) * ZC] = tile
+                hids[(v + 1) * CIN : (v + 2) * CIN, (y - v) * ZC : (y - v + 1) * ZC] = tile
     none = jnp.zeros((CIN, ZC), jnp.bfloat16)
-    hid_ref[0:CIN, 0:ZC] = none
-    hid_ref[2 * CIN : 3 * CIN, (YC - 1) * ZC : YC * ZC] = none
+    hids[0:CIN, 0:ZC] = none
+    hids[2 * CIN : 3 * CIN, (YC - 1) * ZC : YC * ZC] = none
+
+
+def own_kernel(
+    act_ref, own_ref, w_ref, hid_ref, grad_ref, tap_ref, sum_ref, up_ref, down_ref, wide, acts, mids
+):
+    spread(own_ref, wide, grad_ref, 0)
+    stack_hidden(act_ref[...].astype(jnp.float32), acts, hid_ref)
     for v in range(3):
         for w in range(3):
             rows, lanes = slice(v * CIN, (v + 1) * CIN), slice(w * COUT, (w + 1) * COUT)
+            down_ref[rows, lanes] = w_ref[3 * v + w]
             mids[rows, lanes] = w_ref[9 + 3 * v + w]
-            side_ref[rows, lanes] = w_ref[3 * v + w]
-            side_ref[rows, (w + 3) * COUT : (w + 4) * COUT] = w_ref[18 + 3 * v + w]
-    tap_ref[...] = by_taps(hid_ref, grads)
-    sum_ref[...] = by_cells(mids, grads)
+            up_ref[rows, lanes] = w_ref[18 + 3 * v + w]
+    tap_ref[...] = by_taps(hid_ref, grad_ref)
+    sum_ref[...] = by_cells(mids, grad_ref)
 
 
 def side_kernel(
-    factor, act_ref, low_ref, high_ref, hid_ref, tap_ref, sum_ref, side_ref, sent_ref, gin_ref, wide, acts, grads
+    factor, act_ref, low_ref, hid_ref, grad_ref, tap_ref, sent_ref, moved_ref, wide, acts, hids
 ):
-    spread(high_ref, wide, grads, 0)
-    spread(low_ref, wide, grads, 3 * COUT)
-    outer = by_taps(hid_ref, grads)
-    inner = tap_ref[...]
-    most = jnp.maximum(
-        jnp.max(jnp.abs(outer), keepdims=True), jnp.max(jnp.abs(inner), keepdims=True)
-    )
+    spread(low_ref, wide, moved_ref, 0)
+    stack_hidden(act_ref[...].astype(jnp.float32), acts, hids)
+    taps = (by_taps(hids, grad_ref), tap_ref[...], by_taps(hid_ref, moved_ref))
+    most = functools.reduce(jnp.maximum, [jnp.max(jnp.abs(t), keepdims=True) for t in taps])
     exponent = jnp.floor(jnp.log2(jnp.maximum(most * factor, 1e-30))) + 1.0
     scale = jnp.broadcast_to(jnp.exp2(TOP - exponent) * factor, (CIN, COUT))
     for x in range(XS):
-        sent_ref[x, XROWS : XROWS + MARKS, :] = jnp.broadcast_to(exponent, (MARKS, COUT))
+        sent_ref[x, XROWS : XROWS + XMARKS, :] = jnp.broadcast_to(exponent, (XMARKS, COUT))
     for tap in range(TAPS):
         u, v, w = tap // 9, tap // 3 % 3, tap % 3
-        rows = slice(v * CIN, (v + 1) * CIN)
-        if u == 1:
-            block = inner[rows, w * COUT : (w + 1) * COUT]
-        else:
-            lane = (u // 2 * 3 + w) * COUT
-            block = outer[rows, lane : lane + COUT]
-        block = block * scale
+        block = taps[u][v * CIN : (v + 1) * CIN, w * COUT : (w + 1) * COUT] * scale
         first = tap * CIN
         while first < (tap + 1) * CIN:
             x = first // XROWS
             last = min((tap + 1) * CIN, (x + 1) * XROWS)
             sent_ref[x, first - x * XROWS : last - x * XROWS, :] = block[first - tap * CIN : last - tap * CIN]
             first = last
-    sums = by_cells(side_ref, grads) + sum_ref[...]
+
+
+def grad_kernel(act_ref, high_ref, moved_ref, sum_ref, up_ref, down_ref, gin_ref, wide, acts, grads):
+    spread(high_ref, wide, grads, 0)
+    sums = by_cells(down_ref, grads) + by_cells(up_ref, moved_ref) + sum_ref[...]
     for y in range(YC):
         total = sums[CIN : 2 * CIN, y * ZC : (y + 1) * ZC]
         if y + 1 < YC:
@@ -122,7 +122,7 @@
         row = 9 * (part // 4) + 2 * (part % 4)
         for i in range(PART):
             sent_ref[part, i * ZS : (i + 1) * ZS, :] = total[pl.ds(row + i, ZS, stride=ZROWS), :]
-        sent_ref[part, PART * ZS : PART * ZS + 12, :] = jnp.broadcast_to(largest, (12, COUT))
+        sent_ref[part, PART * ZS : PART * ZS + YMARKS, :] = jnp.broadcast_to(largest, (YMARKS, COUT))
 
 
 def after_y_kernel(got_ref, sent_ref):
@@ -180,31 +180,43 @@
     act = pre_act.reshape(CIN, YC, ZC)
     own = grad_out.reshape(COUT, YC, ZC)
     low = lax.ppermute(own, "space", forward)
-    high = lax.ppermute(own, "space", backward)
+    low_act = lax.ppermute(act, "space", forward)
     plane = ((COUT * YC, ZC), f32)
     small = ((CIN * YC, ZC), f32)
-    hids, taps, sums, sides = call(
+    stacked, moved, third = ((3 * CIN, CELLS), bf16), ((3 * COUT, CELLS), bf16), ((3 * CIN, 3 * COUT), bf16)
+    hids, grads, taps, sums, up, down = call(
         own_kernel,
         "own_plane",
-        [((3 * CIN, CELLS), bf16), ((3 * CIN, 3 * COUT), f32), ((3 * CIN, CELLS), f32), ((3 * CIN, 6 * COUT), bf16)],
-        [plane, small, ((3 * COUT, CELLS), bf16), ((3 * CIN, 3 * COUT), bf16)],
+        [stacked, moved, ((3 * CIN, 3 * COUT), f32), ((3 * CIN, CELLS), f32), third, third],
+        [plane, small, third],
         1_000_000_000,
         act, own, weight,
     )
-    sent, grad_in = call(
+    sent, low_grads = call(
         functools.partial(side_kernel, factor),
         "side_planes",
-        [((XS, XROWS + MARKS, COUT), f32), ((CIN, YC, ZC), bf16)],
-        [plane, small, ((6 * COUT, CELLS), bf16)],
-        2_000_000_000,
-        act, low, high, hids, taps, sums, sides,
+        [((XS, XROWS + XMARKS, COUT), f32), moved],
+        [plane, small, stacked],
+        1_000_000_000,
+        low_act, low, hids, grads, taps,
     )
     got = exchanged(sent.astype(f16), "space", along_x).astype(f32)
     (sent,) = call(
-        after_x_kernel, "after_x", [((YCS, PART * ZS + 12, COUT), f32)], [((XROWS, COUT), f32)], 1_000_000, got
-    )
+        after_x_kernel, "after_x", [((YCS, PART * ZS + YMARKS, COUT), f32)], [((XROWS, COUT), f32)], 1_000_000, got
+    )
+    own, sent = lax.optimization_barrier((own, sent))
+    high = lax.ppermute(own, "space", backward)
     got = exchanged(sent.astype(f16), "batch", along_y).astype(f32)
     (sent,) = call(after_y_kernel, "after_y", [((ZS, PART, COUT), f32)], [], 1_000_000, got)
+    high, sent = lax.optimization_barrier((high, sent))
+    (grad_in,) = call(
+        grad_kernel,
+        "grad_planes",
+        [((CIN, YC, ZC), bf16)],
+        [plane, small, moved],
+        2_000_000_000,
+        act, high, low_grads, sums, up, down,
+    )
     got = exchanged(sent, ("space", "batch"), along_z)
     total = jnp.sum(got, axis=0).reshape(-1)
     start = (lax.axis_index("batch") & 3) * 32

time: 79.9 us -> 76.9 us (0.962)
  blocking collectives: 38.3 us -> 20.8 us
  starting transfers between devices: 21.2 us -> 30.4 us
  waiting for transfers between devices: 11.9 us -> 15.8 us
    all_to_all x2 -> x1, blocking collectives: 38.3 us -> 20.8 us  [exchanged(): return lax.all_to_all(x, axis, 0, 0, tiled=True, axis_index_groups=members)]
    all_to_all x1 -> x2, waiting for transfers between devices: 8.97 us -> 15.8 us  [exchanged(): return lax.all_to_all(x, axis, 0, 0, tiled=True, axis_index_groups=members)]
    all_to_all x1 -> x2, starting transfers between devices: 15.1 us -> 20.2 us  [exchanged(): return lax.all_to_all(x, axis, 0, 0, tiled=True, axis_index_groups=members)]
    ppermute x0 -> x1, starting transfers between devices: none -> 3.99 us  [on_device(): low_act = lax.ppermute(act, 'space', forward)]
    ppermute x1, waiting for transfers between devices: 2.92 us -> 0.01 us  [on_device(): high = lax.ppermute(own, 'space', backward)]
    pallas_call x4 -> x5, Pallas kernels: 3.61 us -> 3.94 us  [call(): pl.pallas_call(body, out_shape=tuple((jax.ShapeDtypeStruct(shape, dtype)...]
    unnamed x6 -> x10, local copies, waits for them, and re-layouts: 2.86 us -> 2.87 us
  transfers between devices with their start and end apart: 3 -> 5, of which waited for: 2 -> 2; matrix products, arithmetic and copies ran while one was open for 0% -> 0% of each run, Pallas kernels for 1% -> 4%
where the time goes in v3:
time: 76.9 us; the launch traced here: 76 us
  starting transfers between devices  30.4 us (40%)
  blocking collectives  20.8 us (27%)
  waiting for transfers between devices  15.8 us (21%)
  Pallas kernels  3.94 us (5%)
  local copies, waits for them, and re-layouts  3.52 us (5%)
  other arithmetic  0.85 us (1%)
    all_to_all x1, blocking collectives, exchanged(): return lax.all_to_all(x, axis, 0, 0, tiled=True, axis_index_groups=members)  20.8 us
    all_to_all x2, starting transfers between devices, exchanged(): return lax.all_to_all(x, axis, 0, 0, tiled=True, axis_index_groups=members)  20.2 us
    all_to_all x2, waiting for transfers between devices, exchanged(): return lax.all_to_all(x, axis, 0, 0, tiled=True, axis_index_groups=members)  15.8 us
    ppermute x1, starting transfers between devices, on_device(): low = lax.ppermute(own, 'space', forward)  4.83 us
    ppermute x1, starting transfers between devices, on_device(): low_act = lax.ppermute(act, 'space', forward)  3.99 us
    pallas_call x5, Pallas kernels, call(): pl.pallas_call(body, out_shape=tuple((jax.ShapeDtypeStruct(shape, dtype)...  3.94 us
    unnamed x10, local copies, waits for them, and re-layouts  2.87 us
  transfers between devices with their start and end apart: 5, of which 2 were waited for; matrix products, arithmetic and copies ran while one was open for 0% of the time, Pallas kernels for 4%

profile of v3, /device:TPU:1, one launch (start us, length us, event | category | flops | bytes accessed | tf_op | source)
XLA Modules:
  0.0 76.0 jit_solution(11821064418024221667)
XLA Ops:
  0.6 4.8 %collective-permute-start.1 = (bf16[128,8,128]{2,1,0:T(8,128)(2,1)}, bf16[128,8,128]{2,1,0:T(8,128)(2,1)S(1)}, u32[]{:S(2)}, u32[]{:S(2)}) collective-permute-start(bf16[128,8,128]{2,1,0:T(8,128)(2,1)} %bitcast.6), channel_id=1, source_target_pairs={{0,32},{32,64},{64,96},{96,128},{128,160},{160,192},{192,224},{224... | collective-permute-start | bytes 786440 | tf_op jit(solution)/shard_map/ppermute | solution.py:182
  5.5 4.0 %collective-permute-start = (bf16[64,8,128]{2,1,0:T(8,128)(2,1)}, bf16[64,8,128]{2,1,0:T(8,128)(2,1)S(1)}, u32[]{:S(2)}, u32[]{:S(2)}) collective-permute-start(bf16[64,8,128]{2,1,0:T(8,128)(2,1)} %bitcast.9), channel_id=1, source_target_pairs={{0,32},{32,64},{64,96},{96,128},{128,160},{160,192},{192,224},{224... | collective-permute-start | bytes 393224 | tf_op jit(solution)/shard_map/ppermute | solution.py:183
  9.5 0.0 copy-start
  9.5 1.0 %copy-done = bf16[27,64,128]{2,1,0:T(8,128)(2,1)S(1)} copy-done((bf16[27,64,128]{2,1,0:T(8,128)(2,1)S(1)}, bf16[27,64,128]{2,1,0:T(8,128)(2,1)}, u32[]{:S(2)}) %copy-start) | copy-done | bytes 442392
  10.5 0.0 copy-start.1
  10.5 0.9 %copy-done.1 = bf16[1,128,1,8,128]{4,3,2,1,0:T(8,128)(2,1)S(1)} copy-done((bf16[1,128,1,8,128]{4,3,2,1,0:T(8,128)(2,1)S(1)}, bf16[1,128,1,8,128]{4,3,2,1,0:T(8,128)(2,1)}, u32[]{:S(2)}) %copy-start.1) | copy-done | bytes 262168
  11.4 0.0 copy-start.3
  11.4 0.9 %copy-done.3 = bf16[1,64,1,8,128]{4,3,2,1,0:T(8,128)(2,1)S(1)} copy-done((bf16[1,64,1,8,128]{4,3,2,1,0:T(8,128)(2,1)S(1)}, bf16[1,64,1,8,128]{4,3,2,1,0:T(8,128)(2,1)}, u32[]{:S(2)}) %copy-start.3) | copy-done | bytes 131096
  12.3 0.8 %own_plane.1 = (bf16[192,1024]{1,0:T(8,128)(2,1)S(1)}, bf16[384,1024]{1,0:T(8,128)(2,1)S(1)}, f32[192,384]{1,0:T(8,128)S(1)}, f32[192,1024]{1,0:T(8,128)S(1)}, b...) custom-call(bf16[64,8,128]{2,1,0:T(8,128)(2,1)S(1)} %bitcast.10, bf16[128,8,128]{2,1,0:T(8,128)(2,1)S(1)} %bitcast.7, ...), custom_call_target="tpu_custom_call" | custom-call | flops 1000000000 | bytes 2000000 | tf_op jit(solution)/shard_map/own_plane/pallas_call | solution.py:139
  13.2 0.0 collective-permute-done.act_ref
  13.2 0.0 collective-permute-done.1.low_ref
  13.2 1.0 %side_planes.1 = (f32[4,440,128]{2,1,0:T(8,128)S(1)}, bf16[384,1024]{1,0:T(8,128)(2,1)S(1)}) custom-call(bf16[64,8,128]{2,1,0:T(8,128)(2,1)S(1)} %collective-permute-done.act_ref, bf16[128,8,128]{2,1,0:T(8,128)(2,1)S(1)} %collective-permute-done.1.low_ref, bf16[192,1024]{1,0:T(8,128)(2,1)S(1)} %get-tuple-element.14.hid_ref, ...), custom_call_target="tpu_custom_call" | custom-call | flops 1000000000 | bytes 2000000 | tf_op jit(solution)/shard_map/side_planes/pallas_call | solution.py:139
  14.2 0.1 convert_element_type.12
  14.3 20.8 %all_to_all.15 = f16[4,440,128]{2,1,0:T(8,128)(2,1)S(1)} all-to-all(f16[4,440,128]{2,1,0:T(8,128)(2,1)S(1)} %convert_element_type.12), channel_id=1, replica_groups={{0,192,384,576},{32,224,416,608},{64,256,448,640},{96,288,480,672},{128..., dimensions={0} | all-to-all | bytes 901120 | tf_op jit(solution)/shard_map/all_to_all | solution.py:168
  35.0 0.1 convert_element_type.13.got_ref
  35.1 0.1 after_x.1
  35.2 0.7 convert_element_type.14
  35.9 0.0 copy-start.2
  35.9 9.6 %all-to-all-start.1 = ((f16[16,40,128]{2,1,0:T(8,128)(2,1)}), f16[16,40,128]{2,1,0:T(8,128)(2,1)S(1)}, u32[]{:S(2)}, u32[]{:S(2)}) async-start(f16[16,40,128]{2,1,0:T(8,128)(2,1)} %convert_element_type.14), calls=%async_computation.1 | async-start | bytes 327680 | tf_op jit(solution)/shard_map/all_to_all | solution.py:168
  45.6 0.0 copy-done.2
  45.6 1.3 %collective-permute-start.2 = (bf16[128,8,128]{2,1,0:T(8,128)(2,1)S(1)}, bf16[128,8,128]{2,1,0:T(8,128)(2,1)S(1)}, u32[]{:S(2)}, u32[]{:S(2)}) collective-permute-start(bf16[128,8,128]{2,1,0:T(8,128)(2,1)S(1)} %bitcast.8), channel_id=1, source_target_pairs={{32,0},{64,32},{96,64},{128,96},{160,128},{192,160},{224,192},{256... | collective-permute-start | bytes 786440 | tf_op jit(solution)/shard_map/ppermute | solution.py:208
  46.9 8.2 %all-to-all-done.1 = f16[16,40,128]{2,1,0:T(8,128)(2,1)S(1)} async-done(((f16[16,40,128]{2,1,0:T(8,128)(2,1)}), f16[16,40,128]{2,1,0:T(8,128)(2,1)S(1)}, u32[]{:S(2)}, u32[]{:S(2)}) %all-to-all-start.1) | async-done | bytes 163872 | tf_op jit(solution)/shard_map/all_to_all | solution.py:168
  55.1 0.0 copy-start.4
  55.1 0.7 after_y.1
  55.8 0.0 collective-permute-done.2.high_ref
  55.8 10.6 %all-to-all-start.2 = ((f32[12,3,128]{2,1,0:T(4,128)}), f32[12,3,128]{2,1,0:T(4,128)S(1)}, u32[]{:S(2)}, u32[]{:S(2)}) async-start(f32[12,3,128]{2,1,0:T(4,128)} %after_y.1), calls=%async_computation.2 | async-start | bytes 49152 | tf_op jit(solution)/shard_map/all_to_all | solution.py:168
  66.4 0.0 copy-done.4
  66.4 1.3 %grad_planes.1 = bf16[64,8,128]{2,1,0:T(8,128)(2,1)} custom-call(bf16[64,8,128]{2,1,0:T(8,128)(2,1)S(1)} %bitcast.11, bf16[128,8,128]{2,1,0:T(8,128)(2,1)S(1)} %collective-permute-done.2.high_ref, bf16[384,1024]{1,0:T(8,128)(2,1)S(1)} %get-tuple-element.21.moved_ref, f32[192,1024]{1,0:T(8,128)S(1)} %get-tuple-element.22.sum_ref, ...), custom_call_target="tpu_custom_call" | custom-call | flops 2000000000 | bytes 2000000 | tf_op jit(solution)/shard_map/grad_planes/pallas_call | solution.py:139
  67.7 7.6 %all-to-all-done.2 = f32[12,3,128]{2,1,0:T(4,128)S(1)} async-done(((f32[12,3,128]{2,1,0:T(4,128)}), f32[12,3,128]{2,1,0:T(4,128)S(1)}, u32[]{:S(2)}, u32[]{:S(2)}) %all-to-all-start.2) | async-done | bytes 18464 | tf_op jit(solution)/shard_map/all_to_all | solution.py:168
  75.4 0.7 dynamic_slice.3
  (2 shorter events, 0.0 us)
Async XLA Ops:
  0.6 12.6 %collective-permute-start.1 = (bf16[128,8,128]{2,1,0:T(8,128)(2,1)}, bf16[128,8,128]{2,1,0:T(8,128)(2,1)S(1)}, u32[]{:S(2)}, u32[]{:S(2)}) collective-permute-start(bf16[128,8,128]{2,1,0:T(8,128)(2,1)} %bitcast.6), channel_id=1, source_target_pairs={{0,32},{32,64},{64,96},{96,128},{128,160},{160,192},{192,224},{224... | collective-permute-start | bytes 786440 | tf_op jit(solution)/shard_map/ppermute | solution.py:182
  5.5 7.7 %collective-permute-start = (bf16[64,8,128]{2,1,0:T(8,128)(2,1)}, bf16[64,8,128]{2,1,0:T(8,128)(2,1)S(1)}, u32[]{:S(2)}, u32[]{:S(2)}) collective-permute-start(bf16[64,8,128]{2,1,0:T(8,128)(2,1)} %bitcast.9), channel_id=1, source_target_pairs={{0,32},{32,64},{64,96},{96,128},{128,160},{160,192},{192,224},{224... | collective-permute-start | bytes 393224 | tf_op jit(solution)/shard_map/ppermute | solution.py:183
  9.5 1.0 %copy-start = (bf16[27,64,128]{2,1,0:T(8,128)(2,1)S(1)}, bf16[27,64,128]{2,1,0:T(8,128)(2,1)}, u32[]{:S(2)}) copy-start(bf16[27,64,128]{2,1,0:T(8,128)(2,1)} %w_ref.1) | copy-start | bytes 1327108
  10.5 0.9 %copy-start.1 = (bf16[1,128,1,8,128]{4,3,2,1,0:T(8,128)(2,1)S(1)}, bf16[1,128,1,8,128]{4,3,2,1,0:T(8,128)(2,1)}, u32[]{:S(2)}) copy-start(bf16[1,128,1,8,128]{4,3,2,1,0:T(8,128)(2,1)} %param.4) | copy-start | bytes 786436
  11.4 0.9 %copy-start.3 = (bf16[1,64,1,8,128]{4,3,2,1,0:T(8,128)(2,1)S(1)}, bf16[1,64,1,8,128]{4,3,2,1,0:T(8,128)(2,1)}, u32[]{:S(2)}) copy-start(bf16[1,64,1,8,128]{4,3,2,1,0:T(8,128)(2,1)} %param.3) | copy-start | bytes 393220
  35.9 9.6 %copy-start.2 = (bf16[1,128,1,8,128]{4,3,2,1,0:T(8,128)(2,1)S(1)}, bf16[1,128,1,8,128]{4,3,2,1,0:T(8,128)(2,1)}, u32[]{:S(2)}) copy-start(bf16[1,128,1,8,128]{4,3,2,1,0:T(8,128)(2,1)} %param.4) | copy-start | bytes 786436
  35.9 19.2 %all-to-all-start.1 = ((f16[16,40,128]{2,1,0:T(8,128)(2,1)}), f16[16,40,128]{2,1,0:T(8,128)(2,1)S(1)}, u32[]{:S(2)}, u32[]{:S(2)}) async-start(f16[16,40,128]{2,1,0:T(8,128)(2,1)} %convert_element_type.14), calls=%async_computation.1 | async-start | bytes 327680 | tf_op jit(solution)/shard_map/all_to_all | solution.py:168
  45.6 10.2 %collective-permute-start.2 = (bf16[128,8,128]{2,1,0:T(8,128)(2,1)S(1)}, bf16[128,8,128]{2,1,0:T(8,128)(2,1)S(1)}, u32[]{:S(2)}, u32[]{:S(2)}) collective-permute-start(bf16[128,8,128]{2,1,0:T(8,128)(2,1)S(1)} %bitcast.8), channel_id=1, source_target_pairs={{32,0},{64,32},{96,64},{128,96},{160,128},{192,160},{224,192},{256... | collective-permute-start | bytes 786440 | tf_op jit(solution)/shard_map/ppermute | solution.py:208
  55.1 11.3 %copy-start.4 = (bf16[1,64,1,8,128]{4,3,2,1,0:T(8,128)(2,1)S(1)}, bf16[1,64,1,8,128]{4,3,2,1,0:T(8,128)(2,1)}, u32[]{:S(2)}) copy-start(bf16[1,64,1,8,128]{4,3,2,1,0:T(8,128)(2,1)} %param.3) | copy-start | bytes 393220
  55.8 19.6 %all-to-all-start.2 = ((f32[12,3,128]{2,1,0:T(4,128)}), f32[12,3,128]{2,1,0:T(4,128)S(1)}, u32[]{:S(2)}, u32[]{:S(2)}) async-start(f32[12,3,128]{2,1,0:T(4,128)} %after_y.1), calls=%async_computation.2 | async-start | bytes 49152 | tf_op jit(solution)/shard_map/all_to_all | solution.py:168

commit v4 on v3

--- a/solution.py
+++ b/solution.py
@@ -208,7 +208,7 @@
     high = lax.ppermute(own, "space", backward)
     got = exchanged(sent.astype(f16), "batch", along_y).astype(f32)
     (sent,) = call(after_y_kernel, "after_y", [((ZS, PART, COUT), f32)], [], 1_000_000, got)
-    high, sent = lax.optimization_barrier((high, sent))
+    sums, _ = lax.optimization_barrier((sums, sent))
     (grad_in,) = call(
         grad_kernel,
         "grad_planes",

time: 76.9 us -> 76.5 us (level)
  no operation moved by 1% of the time
where the time goes in v4:
time: 76.5 us; the launch traced here: 76 us
  starting transfers between devices  30.4 us (40%)
  blocking collectives  20.8 us (27%)
  waiting for transfers between devices  15.8 us (21%)
  Pallas kernels  3.95 us (5%)
  local copies, waits for them, and re-layouts  3.52 us (5%)
  other arithmetic  0.85 us (1%)
    all_to_all x1, blocking collectives, exchanged(): return lax.all_to_all(x, axis, 0, 0, tiled=True, axis_index_groups=members)  20.8 us
    all_to_all x2, starting transfers between devices, exchanged(): return lax.all_to_all(x, axis, 0, 0, tiled=True, axis_index_groups=members)  20.2 us
    all_to_all x2, waiting for transfers between devices, exchanged(): return lax.all_to_all(x, axis, 0, 0, tiled=True, axis_index_groups=members)  15.8 us
    ppermute x1, starting transfers between devices, on_device(): low = lax.ppermute(own, 'space', forward)  4.83 us
    ppermute x1, starting transfers between devices, on_device(): low_act = lax.ppermute(act, 'space', forward)  3.99 us
    pallas_call x5, Pallas kernels, call(): pl.pallas_call(body, out_shape=tuple((jax.ShapeDtypeStruct(shape, dtype)...  3.95 us
    unnamed x10, local copies, waits for them, and re-layouts  2.87 us
  transfers between devices with their start and end apart: 5, of which 2 were waited for; matrix products, arithmetic and copies ran while one was open for 0% of the time, Pallas kernels for 4%

profile of v4, /device:TPU:1, one launch (start us, length us, event | category | flops | bytes accessed | tf_op | source)
XLA Modules:
  0.0 76.0 jit_solution(10258743889360229006)
XLA Ops:
  0.6 4.8 %collective-permute-start.1 = (bf16[128,8,128]{2,1,0:T(8,128)(2,1)}, bf16[128,8,128]{2,1,0:T(8,128)(2,1)S(1)}, u32[]{:S(2)}, u32[]{:S(2)}) collective-permute-start(bf16[128,8,128]{2,1,0:T(8,128)(2,1)} %bitcast.6), channel_id=1, source_target_pairs={{0,32},{32,64},{64,96},{96,128},{128,160},{160,192},{192,224},{224... | collective-permute-start | bytes 786440 | tf_op jit(solution)/shard_map/ppermute | solution.py:182
  5.5 4.0 %collective-permute-start = (bf16[64,8,128]{2,1,0:T(8,128)(2,1)}, bf16[64,8,128]{2,1,0:T(8,128)(2,1)S(1)}, u32[]{:S(2)}, u32[]{:S(2)}) collective-permute-start(bf16[64,8,128]{2,1,0:T(8,128)(2,1)} %bitcast.9), channel_id=1, source_target_pairs={{0,32},{32,64},{64,96},{96,128},{128,160},{160,192},{192,224},{224... | collective-permute-start | bytes 393224 | tf_op jit(solution)/shard_map/ppermute | solution.py:183
  9.5 0.0 copy-start
  9.5 1.0 %copy-done = bf16[27,64,128]{2,1,0:T(8,128)(2,1)S(1)} copy-done((bf16[27,64,128]{2,1,0:T(8,128)(2,1)S(1)}, bf16[27,64,128]{2,1,0:T(8,128)(2,1)}, u32[]{:S(2)}) %copy-start) | copy-done | bytes 442392
  10.5 0.0 copy-start.1
  10.5 0.9 %copy-done.1 = bf16[1,128,1,8,128]{4,3,2,1,0:T(8,128)(2,1)S(1)} copy-done((bf16[1,128,1,8,128]{4,3,2,1,0:T(8,128)(2,1)S(1)}, bf16[1,128,1,8,128]{4,3,2,1,0:T(8,128)(2,1)}, u32[]{:S(2)}) %copy-start.1) | copy-done | bytes 262168
  11.4 0.0 copy-start.3
  11.4 0.9 %copy-done.3 = bf16[1,64,1,8,128]{4,3,2,1,0:T(8,128)(2,1)S(1)} copy-done((bf16[1,64,1,8,128]{4,3,2,1,0:T(8,128)(2,1)S(1)}, bf16[1,64,1,8,128]{4,3,2,1,0:T(8,128)(2,1)}, u32[]{:S(2)}) %copy-start.3) | copy-done | bytes 131096
  12.3 0.8 %own_plane.1 = (bf16[192,1024]{1,0:T(8,128)(2,1)S(1)}, bf16[384,1024]{1,0:T(8,128)(2,1)S(1)}, f32[192,384]{1,0:T(8,128)S(1)}, f32[192,1024]{1,0:T(8,128)S(1)}, b...) custom-call(bf16[64,8,128]{2,1,0:T(8,128)(2,1)S(1)} %bitcast.10, bf16[128,8,128]{2,1,0:T(8,128)(2,1)S(1)} %bitcast.7, ...), custom_call_target="tpu_custom_call" | custom-call | flops 1000000000 | bytes 2000000 | tf_op jit(solution)/shard_map/own_plane/pallas_call | solution.py:139
  13.2 0.0 collective-permute-done.act_ref
  13.2 0.0 collective-permute-done.1.low_ref
  13.2 1.0 %side_planes.1 = (f32[4,440,128]{2,1,0:T(8,128)S(1)}, bf16[384,1024]{1,0:T(8,128)(2,1)S(1)}) custom-call(bf16[64,8,128]{2,1,0:T(8,128)(2,1)S(1)} %collective-permute-done.act_ref, bf16[128,8,128]{2,1,0:T(8,128)(2,1)S(1)} %collective-permute-done.1.low_ref, bf16[192,1024]{1,0:T(8,128)(2,1)S(1)} %get-tuple-element.13.hid_ref, ...), custom_call_target="tpu_custom_call" | custom-call | flops 1000000000 | bytes 2000000 | tf_op jit(solution)/shard_map/side_planes/pallas_call | solution.py:139
  14.2 0.1 convert_element_type.12
  14.3 20.8 %all_to_all.15 = f16[4,440,128]{2,1,0:T(8,128)(2,1)S(1)} all-to-all(f16[4,440,128]{2,1,0:T(8,128)(2,1)S(1)} %convert_element_type.12), channel_id=1, replica_groups={{0,192,384,576},{32,224,416,608},{64,256,448,640},{96,288,480,672},{128..., dimensions={0} | all-to-all | bytes 901120 | tf_op jit(solution)/shard_map/all_to_all | solution.py:168
  35.0 0.1 convert_element_type.13.got_ref
  35.1 0.1 after_x.1
  35.2 0.7 convert_element_type.14
  35.9 0.0 copy-start.2
  35.9 9.6 %all-to-all-start.1 = ((f16[16,40,128]{2,1,0:T(8,128)(2,1)}), f16[16,40,128]{2,1,0:T(8,128)(2,1)S(1)}, u32[]{:S(2)}, u32[]{:S(2)}) async-start(f16[16,40,128]{2,1,0:T(8,128)(2,1)} %convert_element_type.14), calls=%async_computation.1 | async-start | bytes 327680 | tf_op jit(solution)/shard_map/all_to_all | solution.py:168
  45.6 0.0 copy-done.2
  45.6 1.3 %collective-permute-start.2 = (bf16[128,8,128]{2,1,0:T(8,128)(2,1)S(1)}, bf16[128,8,128]{2,1,0:T(8,128)(2,1)S(1)}, u32[]{:S(2)}, u32[]{:S(2)}) collective-permute-start(bf16[128,8,128]{2,1,0:T(8,128)(2,1)S(1)} %bitcast.8), channel_id=1, source_target_pairs={{32,0},{64,32},{96,64},{128,96},{160,128},{192,160},{224,192},{256... | collective-permute-start | bytes 786440 | tf_op jit(solution)/shard_map/ppermute | solution.py:208
  46.9 8.2 %all-to-all-done.1 = f16[16,40,128]{2,1,0:T(8,128)(2,1)S(1)} async-done(((f16[16,40,128]{2,1,0:T(8,128)(2,1)}), f16[16,40,128]{2,1,0:T(8,128)(2,1)S(1)}, u32[]{:S(2)}, u32[]{:S(2)}) %all-to-all-start.1) | async-done | bytes 163872 | tf_op jit(solution)/shard_map/all_to_all | solution.py:168
  55.1 0.0 copy-start.4
  55.1 0.7 after_y.1
  55.8 10.6 %all-to-all-start.2 = ((f32[12,3,128]{2,1,0:T(4,128)}), f32[12,3,128]{2,1,0:T(4,128)S(1)}, u32[]{:S(2)}, u32[]{:S(2)}) async-start(f32[12,3,128]{2,1,0:T(4,128)} %after_y.1), calls=%async_computation.2 | async-start | bytes 49152 | tf_op jit(solution)/shard_map/all_to_all | solution.py:168
  66.4 0.0 collective-permute-done.2.high_ref
  66.4 0.0 copy-done.4
  66.4 1.3 %grad_planes.1 = bf16[64,8,128]{2,1,0:T(8,128)(2,1)} custom-call(bf16[64,8,128]{2,1,0:T(8,128)(2,1)S(1)} %bitcast.11, bf16[128,8,128]{2,1,0:T(8,128)(2,1)S(1)} %collective-permute-done.2.high_ref, bf16[384,1024]{1,0:T(8,128)(2,1)S(1)} %get-tuple-element.18.moved_ref, f32[192,1024]{1,0:T(8,128)S(1)} %get-tuple-element.21.sum_ref, ...), custom_call_target="tpu_custom_call" | custom-call | flops 2000000000 | bytes 2000000 | tf_op jit(solution)/shard_map/grad_planes/pallas_call | solution.py:139
  67.7 7.6 %all-to-all-done.2 = f32[12,3,128]{2,1,0:T(4,128)S(1)} async-done(((f32[12,3,128]{2,1,0:T(4,128)}), f32[12,3,128]{2,1,0:T(4,128)S(1)}, u32[]{:S(2)}, u32[]{:S(2)}) %all-to-all-start.2) | async-done | bytes 18464 | tf_op jit(solution)/shard_map/all_to_all | solution.py:168
  75.4 0.7 dynamic_slice.3
  (2 shorter events, 0.0 us)
Async XLA Ops:
  0.6 12.6 %collective-permute-start.1 = (bf16[128,8,128]{2,1,0:T(8,128)(2,1)}, bf16[128,8,128]{2,1,0:T(8,128)(2,1)S(1)}, u32[]{:S(2)}, u32[]{:S(2)}) collective-permute-start(bf16[128,8,128]{2,1,0:T(8,128)(2,1)} %bitcast.6), channel_id=1, source_target_pairs={{0,32},{32,64},{64,96},{96,128},{128,160},{160,192},{192,224},{224... | collective-permute-start | bytes 786440 | tf_op jit(solution)/shard_map/ppermute | solution.py:182
  5.5 7.7 %collective-permute-start = (bf16[64,8,128]{2,1,0:T(8,128)(2,1)}, bf16[64,8,128]{2,1,0:T(8,128)(2,1)S(1)}, u32[]{:S(2)}, u32[]{:S(2)}) collective-permute-start(bf16[64,8,128]{2,1,0:T(8,128)(2,1)} %bitcast.9), channel_id=1, source_target_pairs={{0,32},{32,64},{64,96},{96,128},{128,160},{160,192},{192,224},{224... | collective-permute-start | bytes 393224 | tf_op jit(solution)/shard_map/ppermute | solution.py:183
  9.5 1.0 %copy-start = (bf16[27,64,128]{2,1,0:T(8,128)(2,1)S(1)}, bf16[27,64,128]{2,1,0:T(8,128)(2,1)}, u32[]{:S(2)}) copy-start(bf16[27,64,128]{2,1,0:T(8,128)(2,1)} %w_ref.1) | copy-start | bytes 1327108
  10.5 0.9 %copy-start.1 = (bf16[1,128,1,8,128]{4,3,2,1,0:T(8,128)(2,1)S(1)}, bf16[1,128,1,8,128]{4,3,2,1,0:T(8,128)(2,1)}, u32[]{:S(2)}) copy-start(bf16[1,128,1,8,128]{4,3,2,1,0:T(8,128)(2,1)} %param.4) | copy-start | bytes 786436
  11.4 0.9 %copy-start.3 = (bf16[1,64,1,8,128]{4,3,2,1,0:T(8,128)(2,1)S(1)}, bf16[1,64,1,8,128]{4,3,2,1,0:T(8,128)(2,1)}, u32[]{:S(2)}) copy-start(bf16[1,64,1,8,128]{4,3,2,1,0:T(8,128)(2,1)} %param.3) | copy-start | bytes 393220
  35.9 9.6 %copy-start.2 = (bf16[1,128,1,8,128]{4,3,2,1,0:T(8,128)(2,1)S(1)}, bf16[1,128,1,8,128]{4,3,2,1,0:T(8,128)(2,1)}, u32[]{:S(2)}) copy-start(bf16[1,128,1,8,128]{4,3,2,1,0:T(8,128)(2,1)} %param.4) | copy-start | bytes 786436
  35.9 19.2 %all-to-all-start.1 = ((f16[16,40,128]{2,1,0:T(8,128)(2,1)}), f16[16,40,128]{2,1,0:T(8,128)(2,1)S(1)}, u32[]{:S(2)}, u32[]{:S(2)}) async-start(f16[16,40,128]{2,1,0:T(8,128)(2,1)} %convert_element_type.14), calls=%async_computation.1 | async-start | bytes 327680 | tf_op jit(solution)/shard_map/all_to_all | solution.py:168
  45.6 20.8 %collective-permute-start.2 = (bf16[128,8,128]{2,1,0:T(8,128)(2,1)S(1)}, bf16[128,8,128]{2,1,0:T(8,128)(2,1)S(1)}, u32[]{:S(2)}, u32[]{:S(2)}) collective-permute-start(bf16[128,8,128]{2,1,0:T(8,128)(2,1)S(1)} %bitcast.8), channel_id=1, source_target_pairs={{32,0},{64,32},{96,64},{128,96},{160,128},{192,160},{224,192},{256... | collective-permute-start | bytes 786440 | tf_op jit(solution)/shard_map/ppermute | solution.py:208
  55.1 11.3 %copy-start.4 = (bf16[1,64,1,8,128]{4,3,2,1,0:T(8,128)(2,1)S(1)}, bf16[1,64,1,8,128]{4,3,2,1,0:T(8,128)(2,1)}, u32[]{:S(2)}) copy-start(bf16[1,64,1,8,128]{4,3,2,1,0:T(8,128)(2,1)} %param.3) | copy-start | bytes 393220
  55.8 19.6 %all-to-all-start.2 = ((f32[12,3,128]{2,1,0:T(4,128)}), f32[12,3,128]{2,1,0:T(4,128)S(1)}, u32[]{:S(2)}, u32[]{:S(2)}) async-start(f32[12,3,128]{2,1,0:T(4,128)} %after_y.1), calls=%async_computation.2 | async-start | bytes 49152 | tf_op jit(solution)/shard_map/all_to_all | solution.py:168

commit v5 on v4

--- a/solution.py
+++ b/solution.py
@@ -63,8 +63,9 @@
 
 
 def own_kernel(
-    act_ref, own_ref, w_ref, hid_ref, grad_ref, tap_ref, sum_ref, up_ref, down_ref, wide, acts, mids
+    act_ref, own_ref, w_ref, hid_ref, grad_ref, tap_ref, sum_ref, up_ref, down_ref, kept_ref, wide, acts, mids
 ):
+    kept_ref[...] = own_ref[...]
     spread(own_ref, wide, grad_ref, 0)
     stack_hidden(act_ref[...].astype(jnp.float32), acts, hid_ref)
     for v in range(3):
@@ -114,7 +115,8 @@
     gin_ref[...] = (grad_hidden * jnp.where(act > 0, 1.0, slope)).astype(jnp.bfloat16)
 
 
-def after_x_kernel(got_ref, sent_ref, total):
+def after_x_kernel(got_ref, own_ref, sent_ref, copy_ref, total):
+    copy_ref[...] = own_ref[...]
     exps = [got_ref[i, XROWS : XROWS + 1, :] for i in range(XS)]
     largest = functools.reduce(jnp.maximum, exps) + 2.0
     total[...] = sum(got_ref[i, 0:XROWS, :] * jnp.exp2(exps[i] - largest) for i in range(XS))
@@ -134,7 +136,7 @@
         sent_ref[:, i, :] = total[i * ZS : (i + 1) * ZS]
 
 
-def call(body, name, outs, scratch, flops, *args):
+def call(body, outs, scratch, flops, *args):
     vmem = pl.BlockSpec(memory_space=pltpu.VMEM)
     return pl.pallas_call(
         body,
@@ -144,7 +146,6 @@
         scratch_shapes=[pltpu.VMEM(shape, dtype) for shape, dtype in scratch],
         compiler_params=pltpu.CompilerParams(vmem_limit_bytes=16 * 1024 * 1024),
         cost_estimate=pl.CostEstimate(flops=flops, bytes_accessed=2_000_000, transcendentals=0),
-        name=name,
     )(*args)
 
 
@@ -168,7 +169,7 @@
     return lax.all_to_all(x, axis, 0, 0, tiled=True, axis_index_groups=members)
 
 
-def on_device(pre_act, grad_out, weight):
+def gradients(pre_act, grad_out, weight):
     f32, bf16, f16 = jnp.float32, jnp.bfloat16, jnp.float16
     count = pre_act.shape[0] * lax.axis_size("batch") * lax.axis_size("space") * CELLS
     factor = float(1.0 / count**0.5)
@@ -184,34 +185,35 @@
     plane = ((COUT * YC, ZC), f32)
     small = ((CIN * YC, ZC), f32)
     stacked, moved, third = ((3 * CIN, CELLS), bf16), ((3 * COUT, CELLS), bf16), ((3 * CIN, 3 * COUT), bf16)
-    hids, grads, taps, sums, up, down = call(
+    hids, grads, taps, sums, up, down, kept = call(
         own_kernel,
-        "own_plane",
-        [stacked, moved, ((3 * CIN, 3 * COUT), f32), ((3 * CIN, CELLS), f32), third, third],
+        [stacked, moved, ((3 * CIN, 3 * COUT), f32), ((3 * CIN, CELLS), f32), third, third, ((COUT, YC, ZC), bf16)],
         [plane, small, third],
         1_000_000_000,
         act, own, weight,
     )
     sent, low_grads = call(
         functools.partial(side_kernel, factor),
-        "side_planes",
         [((XS, XROWS + XMARKS, COUT), f32), moved],
         [plane, small, stacked],
         1_000_000_000,
         low_act, low, hids, grads, taps,
     )
     got = exchanged(sent.astype(f16), "space", along_x).astype(f32)
-    (sent,) = call(
-        after_x_kernel, "after_x", [((YCS, PART * ZS + YMARKS, COUT), f32)], [((XROWS, COUT), f32)], 1_000_000, got
-    )
-    own, sent = lax.optimization_barrier((own, sent))
+    sent, own = call(
+        after_x_kernel,
+        [((YCS, PART * ZS + YMARKS, COUT), f32), ((COUT, YC, ZC), bf16)],
+        [((XROWS, COUT), f32)],
+        1_000_000,
+        got, kept,
+    )
     high = lax.ppermute(own, "space", backward)
-    got = exchanged(sent.astype(f16), "batch", along_y).astype(f32)
-    (sent,) = call(after_y_kernel, "after_y", [((ZS, PART, COUT), f32)], [], 1_000_000, got)
+    got = exchanged(sent.astype(f16), "batch", along_y)
+    got = got.astype(f32)
+    (sent,) = call(after_y_kernel, [((ZS, PART, COUT), f32)], [], 1_000_000, got)
     sums, _ = lax.optimization_barrier((sums, sent))
     (grad_in,) = call(
         grad_kernel,
-        "grad_planes",
         [((CIN, YC, ZC), bf16)],
         [plane, small, moved],
         2_000_000_000,
@@ -226,7 +228,7 @@
 
 def solution(mesh):
     return jax.shard_map(
-        on_device,
+        gradients,
         mesh=mesh,
         in_specs=(
             P("batch", None, "space", None, None),

time: 76.5 us -> 76.3 us (level)
    unnamed x10 -> x8, local copies, waits for them, and re-layouts: 2.87 us -> 2.87 us
where the time goes in v5:
time: 76.3 us; the launch traced here: 75.9 us
  starting transfers between devices  30.2 us (40%)
  blocking collectives  20.8 us (27%)
  waiting for transfers between devices  15.8 us (21%)
  Pallas kernels  3.98 us (5%)
  local copies, waits for them, and re-layouts  3.52 us (5%)
  other arithmetic  0.85 us (1%)
    all_to_all x1, blocking collectives, exchanged(): return lax.all_to_all(x, axis, 0, 0, tiled=True, axis_index_groups=members)  20.8 us
    all_to_all x2, starting transfers between devices, exchanged(): return lax.all_to_all(x, axis, 0, 0, tiled=True, axis_index_groups=members)  20.1 us
    all_to_all x2, waiting for transfers between devices, exchanged(): return lax.all_to_all(x, axis, 0, 0, tiled=True, axis_index_groups=members)  15.8 us
    ppermute x1, starting transfers between devices, gradients(): low = lax.ppermute(own, 'space', forward)  4.83 us
    ppermute x1, starting transfers between devices, gradients(): low_act = lax.ppermute(act, 'space', forward)  3.99 us
    pallas_call x5, Pallas kernels, call(): pl.pallas_call(body, out_shape=tuple((jax.ShapeDtypeStruct(shape, dtype)...  3.98 us
    unnamed x8, local copies, waits for them, and re-layouts  2.87 us
  transfers between devices with their start and end apart: 5, of which 2 were waited for; matrix products, arithmetic and copies ran while one was open for 0% of the time, Pallas kernels for 4%

profile of v5, /device:TPU:1, one launch (start us, length us, event | category | flops | bytes accessed | tf_op | source)
XLA Modules:
  0.0 75.9 jit_solution(14479733612986086791)
XLA Ops:
  0.6 4.8 %collective-permute-start.1 = (bf16[128,8,128]{2,1,0:T(8,128)(2,1)}, bf16[128,8,128]{2,1,0:T(8,128)(2,1)S(1)}, u32[]{:S(2)}, u32[]{:S(2)}) collective-permute-start(bf16[128,8,128]{2,1,0:T(8,128)(2,1)} %bitcast.6), channel_id=1, source_target_pairs={{0,32},{32,64},{64,96},{96,128},{128,160},{160,192},{192,224},{224... | collective-permute-start | bytes 786440 | tf_op jit(solution)/shard_map/ppermute | solution.py:183
  5.5 4.0 %collective-permute-start = (bf16[64,8,128]{2,1,0:T(8,128)(2,1)}, bf16[64,8,128]{2,1,0:T(8,128)(2,1)S(1)}, u32[]{:S(2)}, u32[]{:S(2)}) collective-permute-start(bf16[64,8,128]{2,1,0:T(8,128)(2,1)} %bitcast.8), channel_id=1, source_target_pairs={{0,32},{32,64},{64,96},{96,128},{128,160},{160,192},{192,224},{224... | collective-permute-start | bytes 393224 | tf_op jit(solution)/shard_map/ppermute | solution.py:184
  9.5 0.0 copy-start
  9.5 1.0 %copy-done = bf16[27,64,128]{2,1,0:T(8,128)(2,1)S(1)} copy-done((bf16[27,64,128]{2,1,0:T(8,128)(2,1)S(1)}, bf16[27,64,128]{2,1,0:T(8,128)(2,1)}, u32[]{:S(2)}) %copy-start) | copy-done | bytes 442392
  10.5 0.0 copy-start.1
  10.5 0.9 %copy-done.1 = bf16[1,128,1,8,128]{4,3,2,1,0:T(8,128)(2,1)S(1)} copy-done((bf16[1,128,1,8,128]{4,3,2,1,0:T(8,128)(2,1)S(1)}, bf16[1,128,1,8,128]{4,3,2,1,0:T(8,128)(2,1)}, u32[]{:S(2)}) %copy-start.1) | copy-done | bytes 262168
  11.4 0.0 copy-start.2
  11.4 0.9 %copy-done.2 = bf16[1,64,1,8,128]{4,3,2,1,0:T(8,128)(2,1)S(1)} copy-done((bf16[1,64,1,8,128]{4,3,2,1,0:T(8,128)(2,1)S(1)}, bf16[1,64,1,8,128]{4,3,2,1,0:T(8,128)(2,1)}, u32[]{:S(2)}) %copy-start.2) | copy-done | bytes 131096
  12.3 0.9 %shard_map.50 = (bf16[192,1024]{1,0:T(8,128)(2,1)S(1)}, bf16[384,1024]{1,0:T(8,128)(2,1)S(1)}, f32[192,384]{1,0:T(8,128)S(1)}, f32[192,1024]{1,0:T(8,128)S(1)}, ...) custom-call(bf16[64,8,128]{2,1,0:T(8,128)(2,1)S(1)} %bitcast.9, ...), custom_call_target="tpu_custom_call" | custom-call | flops 1000000000 | bytes 2000000 | tf_op jit(solution)/shard_map/pallas_call | solution.py:141
  13.2 0.0 collective-permute-done.act_ref
  13.2 0.0 collective-permute-done.1.low_ref
  13.2 1.0 %shard_map.51 = (f32[4,440,128]{2,1,0:T(8,128)S(1)}, bf16[384,1024]{1,0:T(8,128)(2,1)S(1)}) custom-call(bf16[64,8,128]{2,1,0:T(8,128)(2,1)S(1)} %collective-permute-done.act_ref, bf16[128,8,128]{2,1,0:T(8,128)(2,1)S(1)} %collective-permute-done.1.low_ref, bf16[192,1024]{1,0:T(8,128)(2,1)S(1)} %get-tuple-element.14.hid_ref, ...), custom_call_target="tpu_custom_call" | custom-call | flops 1000000000 | bytes 2000000 | tf_op jit(solution)/shard_map/pallas_call | solution.py:141
  14.2 0.1 convert_element_type.12
  14.3 20.8 %all_to_all.15 = f16[4,440,128]{2,1,0:T(8,128)(2,1)S(1)} all-to-all(f16[4,440,128]{2,1,0:T(8,128)(2,1)S(1)} %convert_element_type.12), channel_id=1, replica_groups={{0,192,384,576},{32,224,416,608},{64,256,448,640},{96,288,480,672},{128..., dimensions={0} | all-to-all | bytes 901120 | tf_op jit(solution)/shard_map/all_to_all | solution.py:169
  35.0 0.1 convert_element_type.13.got_ref
  35.1 0.2 shard_map.52
  35.3 0.7 convert_element_type.14
  35.9 9.5 %all-to-all-start.1 = ((f16[16,40,128]{2,1,0:T(8,128)(2,1)}), f16[16,40,128]{2,1,0:T(8,128)(2,1)S(1)}, u32[]{:S(2)}, u32[]{:S(2)}) async-start(f16[16,40,128]{2,1,0:T(8,128)(2,1)} %convert_element_type.14), calls=%async_computation.1 | async-start | bytes 327680 | tf_op jit(solution)/shard_map/all_to_all | solution.py:169
  45.4 1.3 %collective-permute-start.2 = (bf16[128,8,128]{2,1,0:T(8,128)(2,1)S(1)}, bf16[128,8,128]{2,1,0:T(8,128)(2,1)S(1)}, u32[]{:S(2)}, u32[]{:S(2)}) collective-permute-start(bf16[128,8,128]{2,1,0:T(8,128)(2,1)S(1)} %get-tuple-element.19), channel_id=1, source_target_pairs={{32,0},{64,32},{96,64},{128,96},{160,128},{192,160},{224,192},{256... | collective-permute-start | bytes 786440 | tf_op jit(solution)/shard_map/ppermute | solution.py:210
  46.7 8.2 %all-to-all-done.1 = f16[16,40,128]{2,1,0:T(8,128)(2,1)S(1)} async-done(((f16[16,40,128]{2,1,0:T(8,128)(2,1)}), f16[16,40,128]{2,1,0:T(8,128)(2,1)S(1)}, u32[]{:S(2)}, u32[]{:S(2)}) %all-to-all-start.1) | async-done | bytes 163872 | tf_op jit(solution)/shard_map/all_to_all | solution.py:169
  55.0 0.0 copy-start.3
  55.0 0.7 shard_map.53
  55.7 10.6 %all-to-all-start.2 = ((f32[12,3,128]{2,1,0:T(4,128)}), f32[12,3,128]{2,1,0:T(4,128)S(1)}, u32[]{:S(2)}, u32[]{:S(2)}) async-start(f32[12,3,128]{2,1,0:T(4,128)} %shard_map.53), calls=%async_computation.2 | async-start | bytes 49152 | tf_op jit(solution)/shard_map/all_to_all | solution.py:169
  66.3 0.0 collective-permute-done.2.high_ref
  66.3 0.0 copy-done.3
  66.3 1.3 %shard_map.54 = bf16[64,8,128]{2,1,0:T(8,128)(2,1)} custom-call(bf16[64,8,128]{2,1,0:T(8,128)(2,1)S(1)} %bitcast.10, bf16[128,8,128]{2,1,0:T(8,128)(2,1)S(1)} %collective-permute-done.2.high_ref, bf16[384,1024]{1,0:T(8,128)(2,1)S(1)} %get-tuple-element.20.moved_ref, f32[192,1024]{1,0:T(8,128)S(1)} %get-tuple-element.23.sum_ref, ...), custom_call_target="tpu_custom_call" | custom-call | flops 2000000000 | bytes 2000000 | tf_op jit(solution)/shard_map/pallas_call | solution.py:141
  67.6 7.6 %all-to-all-done.2 = f32[12,3,128]{2,1,0:T(4,128)S(1)} async-done(((f32[12,3,128]{2,1,0:T(4,128)}), f32[12,3,128]{2,1,0:T(4,128)S(1)}, u32[]{:S(2)}, u32[]{:S(2)}) %all-to-all-start.2) | async-done | bytes 18464 | tf_op jit(solution)/shard_map/all_to_all | solution.py:169
  75.3 0.7 dynamic_slice.3
  (2 shorter events, 0.0 us)
Async XLA Ops:
  0.6 12.6 %collective-permute-start.1 = (bf16[128,8,128]{2,1,0:T(8,128)(2,1)}, bf16[128,8,128]{2,1,0:T(8,128)(2,1)S(1)}, u32[]{:S(2)}, u32[]{:S(2)}) collective-permute-start(bf16[128,8,128]{2,1,0:T(8,128)(2,1)} %bitcast.6), channel_id=1, source_target_pairs={{0,32},{32,64},{64,96},{96,128},{128,160},{160,192},{192,224},{224... | collective-permute-start | bytes 786440 | tf_op jit(solution)/shard_map/ppermute | solution.py:183
  5.5 7.7 %collective-permute-start = (bf16[64,8,128]{2,1,0:T(8,128)(2,1)}, bf16[64,8,128]{2,1,0:T(8,128)(2,1)S(1)}, u32[]{:S(2)}, u32[]{:S(2)}) collective-permute-start(bf16[64,8,128]{2,1,0:T(8,128)(2,1)} %bitcast.8), channel_id=1, source_target_pairs={{0,32},{32,64},{64,96},{96,128},{128,160},{160,192},{192,224},{224... | collective-permute-start | bytes 393224 | tf_op jit(solution)/shard_map/ppermute | solution.py:184
  9.5 1.0 %copy-start = (bf16[27,64,128]{2,1,0:T(8,128)(2,1)S(1)}, bf16[27,64,128]{2,1,0:T(8,128)(2,1)}, u32[]{:S(2)}) copy-start(bf16[27,64,128]{2,1,0:T(8,128)(2,1)} %w_ref.1) | copy-start | bytes 1327108
  10.5 0.9 %copy-start.1 = (bf16[1,128,1,8,128]{4,3,2,1,0:T(8,128)(2,1)S(1)}, bf16[1,128,1,8,128]{4,3,2,1,0:T(8,128)(2,1)}, u32[]{:S(2)}) copy-start(bf16[1,128,1,8,128]{4,3,2,1,0:T(8,128)(2,1)} %param.4) | copy-start | bytes 786436
  11.4 0.9 %copy-start.2 = (bf16[1,64,1,8,128]{4,3,2,1,0:T(8,128)(2,1)S(1)}, bf16[1,64,1,8,128]{4,3,2,1,0:T(8,128)(2,1)}, u32[]{:S(2)}) copy-start(bf16[1,64,1,8,128]{4,3,2,1,0:T(8,128)(2,1)} %param.3) | copy-start | bytes 393220
  35.9 19.0 %all-to-all-start.1 = ((f16[16,40,128]{2,1,0:T(8,128)(2,1)}), f16[16,40,128]{2,1,0:T(8,128)(2,1)S(1)}, u32[]{:S(2)}, u32[]{:S(2)}) async-start(f16[16,40,128]{2,1,0:T(8,128)(2,1)} %convert_element_type.14), calls=%async_computation.1 | async-start | bytes 327680 | tf_op jit(solution)/shard_map/all_to_all | solution.py:169
  45.4 20.8 %collective-permute-start.2 = (bf16[128,8,128]{2,1,0:T(8,128)(2,1)S(1)}, bf16[128,8,128]{2,1,0:T(8,128)(2,1)S(1)}, u32[]{:S(2)}, u32[]{:S(2)}) collective-permute-start(bf16[128,8,128]{2,1,0:T(8,128)(2,1)S(1)} %get-tuple-element.19), channel_id=1, source_target_pairs={{32,0},{64,32},{96,64},{128,96},{160,128},{192,160},{224,192},{256... | collective-permute-start | bytes 786440 | tf_op jit(solution)/shard_map/ppermute | solution.py:210
  55.0 11.3 %copy-start.3 = (bf16[1,64,1,8,128]{4,3,2,1,0:T(8,128)(2,1)S(1)}, bf16[1,64,1,8,128]{4,3,2,1,0:T(8,128)(2,1)}, u32[]{:S(2)}) copy-start(bf16[1,64,1,8,128]{4,3,2,1,0:T(8,128)(2,1)} %param.3) | copy-start | bytes 393220
  55.7 19.6 %all-to-all-start.2 = ((f32[12,3,128]{2,1,0:T(4,128)}), f32[12,3,128]{2,1,0:T(4,128)S(1)}, u32[]{:S(2)}, u32[]{:S(2)}) async-start(f32[12,3,128]{2,1,0:T(4,128)} %shard_map.53), calls=%async_computation.2 | async-start | bytes 49152 | tf_op jit(solution)/shard_map/all_to_all | solution.py:169

commit v6 on v5

--- a/solution.py
+++ b/solution.py
@@ -115,8 +115,11 @@
     gin_ref[...] = (grad_hidden * jnp.where(act > 0, 1.0, slope)).astype(jnp.bfloat16)
 
 
-def after_x_kernel(got_ref, own_ref, sent_ref, copy_ref, total):
-    copy_ref[...] = own_ref[...]
+def keep_kernel(own_ref, kept_ref):
+    kept_ref[...] = own_ref[...]
+
+
+def after_x_kernel(got_ref, sent_ref, total):
     exps = [got_ref[i, XROWS : XROWS + 1, :] for i in range(XS)]
     largest = functools.reduce(jnp.maximum, exps) + 2.0
     total[...] = sum(got_ref[i, 0:XROWS, :] * jnp.exp2(exps[i] - largest) for i in range(XS))
@@ -192,6 +195,8 @@
         1_000_000_000,
         act, own, weight,
     )
+    start = (lax.axis_index("batch") & 3) * 32
+    start, taps = lax.optimization_barrier((start, taps))
     sent, low_grads = call(
         functools.partial(side_kernel, factor),
         [((XS, XROWS + XMARKS, COUT), f32), moved],
@@ -199,17 +204,12 @@
         1_000_000_000,
         low_act, low, hids, grads, taps,
     )
-    got = exchanged(sent.astype(f16), "space", along_x).astype(f32)
-    sent, own = call(
-        after_x_kernel,
-        [((YCS, PART * ZS + YMARKS, COUT), f32), ((COUT, YC, ZC), bf16)],
-        [((XROWS, COUT), f32)],
-        1_000_000,
-        got, kept,
-    )
+    got = exchanged(sent.astype(f16), "space", along_x)
+    got = got.astype(f32)
+    (own,) = call(keep_kernel, [((COUT, YC, ZC), bf16)], [], 1_000_000, kept)
     high = lax.ppermute(own, "space", backward)
-    got = exchanged(sent.astype(f16), "batch", along_y)
-    got = got.astype(f32)
+    (sent,) = call(after_x_kernel, [((YCS, PART * ZS + YMARKS, COUT), f32)], [((XROWS, COUT), f32)], 1_000_000, got)
+    got = exchanged(sent.astype(f16), "batch", along_y).astype(f32)
     (sent,) = call(after_y_kernel, [((ZS, PART, COUT), f32)], [], 1_000_000, got)
     sums, _ = lax.optimization_barrier((sums, sent))
     (grad_in,) = call(
@@ -221,7 +221,6 @@
     )
     got = exchanged(sent, ("space", "batch"), along_z)
     total = jnp.sum(got, axis=0).reshape(-1)
-    start = (lax.axis_index("batch") & 3) * 32
     weight_grad = lax.dynamic_slice(total, (start,), (ROWS * COUT // 768,))
     return (grad_in.reshape(pre_act.shape), weight_grad)
 

time: 76.3 us -> 76.3 us (level)
    pallas_call x5 -> x6, Pallas kernels: 3.98 us -> 3.99 us  [call(): pl.pallas_call(body, out_shape=tuple((jax.ShapeDtypeStruct(shape, dtype)...]
where the time goes in v6:
time: 76.3 us; the launch traced here: 75.9 us
  starting transfers between devices  30.2 us (40%)
  blocking collectives  20.8 us (27%)
  waiting for transfers between devices  15.8 us (21%)
  Pallas kernels  3.99 us (5%)
  local copies, waits for them, and re-layouts  3.52 us (5%)
  other arithmetic  0.85 us (1%)
    all_to_all x1, blocking collectives, exchanged(): return lax.all_to_all(x, axis, 0, 0, tiled=True, axis_index_groups=members)  20.8 us
    all_to_all x2, starting transfers between devices, exchanged(): return lax.all_to_all(x, axis, 0, 0, tiled=True, axis_index_groups=members)  20.1 us
    all_to_all x2, waiting for transfers between devices, exchanged(): return lax.all_to_all(x, axis, 0, 0, tiled=True, axis_index_groups=members)  15.8 us
    ppermute x1, starting transfers between devices, gradients(): low = lax.ppermute(own, 'space', forward)  4.83 us
    ppermute x1, starting transfers between devices, gradients(): low_act = lax.ppermute(act, 'space', forward)  3.99 us
    pallas_call x6, Pallas kernels, call(): pl.pallas_call(body, out_shape=tuple((jax.ShapeDtypeStruct(shape, dtype)...  3.99 us
    unnamed x8, local copies, waits for them, and re-layouts  2.87 us
  transfers between devices with their start and end apart: 5, of which 2 were waited for; matrix products, arithmetic and copies ran while one was open for 0% of the time, Pallas kernels for 4%

profile of v6, /device:TPU:1, one launch (start us, length us, event | category | flops | bytes accessed | tf_op | source)
XLA Modules:
  0.0 75.9 jit_solution(17536808413019629644)
XLA Ops:
  0.6 4.8 %collective-permute-start.2 = (bf16[128,8,128]{2,1,0:T(8,128)(2,1)}, bf16[128,8,128]{2,1,0:T(8,128)(2,1)S(1)}, u32[]{:S(2)}, u32[]{:S(2)}) collective-permute-start(bf16[128,8,128]{2,1,0:T(8,128)(2,1)} %bitcast.6), channel_id=1, source_target_pairs={{0,32},{32,64},{64,96},{96,128},{128,160},{160,192},{192,224},{224... | collective-permute-start | bytes 786440 | tf_op jit(solution)/shard_map/ppermute | solution.py:186
  5.5 4.0 %collective-permute-start.1 = (bf16[64,8,128]{2,1,0:T(8,128)(2,1)}, bf16[64,8,128]{2,1,0:T(8,128)(2,1)S(1)}, u32[]{:S(2)}, u32[]{:S(2)}) collective-permute-start(bf16[64,8,128]{2,1,0:T(8,128)(2,1)} %bitcast.8), channel_id=1, source_target_pairs={{0,32},{32,64},{64,96},{96,128},{128,160},{160,192},{192,224},{224... | collective-permute-start | bytes 393224 | tf_op jit(solution)/shard_map/ppermute | solution.py:187
  9.5 0.0 copy-start
  9.5 1.0 %copy-done = bf16[27,64,128]{2,1,0:T(8,128)(2,1)S(1)} copy-done((bf16[27,64,128]{2,1,0:T(8,128)(2,1)S(1)}, bf16[27,64,128]{2,1,0:T(8,128)(2,1)}, u32[]{:S(2)}) %copy-start) | copy-done | bytes 442392
  10.5 0.0 copy-start.1
  10.5 0.9 %copy-done.1 = bf16[1,128,1,8,128]{4,3,2,1,0:T(8,128)(2,1)S(1)} copy-done((bf16[1,128,1,8,128]{4,3,2,1,0:T(8,128)(2,1)S(1)}, bf16[1,128,1,8,128]{4,3,2,1,0:T(8,128)(2,1)}, u32[]{:S(2)}) %copy-start.1) | copy-done | bytes 262168
  11.4 0.0 copy-start.2
  11.4 0.9 %copy-done.2 = bf16[1,64,1,8,128]{4,3,2,1,0:T(8,128)(2,1)S(1)} copy-done((bf16[1,64,1,8,128]{4,3,2,1,0:T(8,128)(2,1)S(1)}, bf16[1,64,1,8,128]{4,3,2,1,0:T(8,128)(2,1)}, u32[]{:S(2)}) %copy-start.2) | copy-done | bytes 131096
  12.3 0.9 %shard_map.50 = (bf16[192,1024]{1,0:T(8,128)(2,1)S(1)}, bf16[384,1024]{1,0:T(8,128)(2,1)S(1)}, f32[192,384]{1,0:T(8,128)S(1)}, f32[192,1024]{1,0:T(8,128)S(1)}, ...) custom-call(bf16[64,8,128]{2,1,0:T(8,128)(2,1)S(1)} %bitcast.9, ...), custom_call_target="tpu_custom_call" | custom-call | flops 1000000000 | bytes 2000000 | tf_op jit(solution)/shard_map/pallas_call | solution.py:144
  13.2 0.0 collective-permute-done.1.act_ref
  13.2 0.0 collective-permute-done.2.low_ref
  13.2 1.0 %shard_map.52 = (f32[4,440,128]{2,1,0:T(8,128)S(1)}, bf16[384,1024]{1,0:T(8,128)(2,1)S(1)}) custom-call(bf16[64,8,128]{2,1,0:T(8,128)(2,1)S(1)} %collective-permute-done.1.act_ref, bf16[128,8,128]{2,1,0:T(8,128)(2,1)S(1)} %collective-permute-done.2.low_ref, bf16[192,1024]{1,0:T(8,128)(2,1)S(1)} %get-tuple-element.15.hid_ref, ...), custom_call_target="tpu_custom_call" | custom-call | flops 1000000000 | bytes 2000000 | tf_op jit(solution)/shard_map/pallas_call | solution.py:144
  14.2 0.1 convert_element_type.12
  14.3 20.8 %all_to_all.15 = f16[4,440,128]{2,1,0:T(8,128)(2,1)S(1)} all-to-all(f16[4,440,128]{2,1,0:T(8,128)(2,1)S(1)} %convert_element_type.12), channel_id=1, replica_groups={{0,192,384,576},{32,224,416,608},{64,256,448,640},{96,288,480,672},{128..., dimensions={0} | all-to-all | bytes 901120 | tf_op jit(solution)/shard_map/all_to_all | solution.py:172
  35.0 0.1 convert_element_type.13.got_ref
  35.1 0.1 shard_map.53
  35.2 0.7 convert_element_type.14
  35.9 9.5 %all-to-all-start.1 = ((f16[16,40,128]{2,1,0:T(8,128)(2,1)}), f16[16,40,128]{2,1,0:T(8,128)(2,1)S(1)}, u32[]{:S(2)}, u32[]{:S(2)}) async-start(f16[16,40,128]{2,1,0:T(8,128)(2,1)} %convert_element_type.14), calls=%async_computation.1 | async-start | bytes 327680 | tf_op jit(solution)/shard_map/all_to_all | solution.py:172
  45.4 1.3 %collective-permute-start = (bf16[128,8,128]{2,1,0:T(8,128)(2,1)S(1)}, bf16[128,8,128]{2,1,0:T(8,128)(2,1)S(1)}, u32[]{:S(2)}, u32[]{:S(2)}) collective-permute-start(bf16[128,8,128]{2,1,0:T(8,128)(2,1)S(1)} %shard_map.51), channel_id=1, source_target_pairs={{32,0},{64,32},{96,64},{128,96},{160,128},{192,160},{224,192},{256... | collective-permute-start | bytes 786440 | tf_op jit(solution)/shard_map/ppermute | solution.py:210
  46.7 8.2 %all-to-all-done.1 = f16[16,40,128]{2,1,0:T(8,128)(2,1)S(1)} async-done(((f16[16,40,128]{2,1,0:T(8,128)(2,1)}), f16[16,40,128]{2,1,0:T(8,128)(2,1)S(1)}, u32[]{:S(2)}, u32[]{:S(2)}) %all-to-all-start.1) | async-done | bytes 163872 | tf_op jit(solution)/shard_map/all_to_all | solution.py:172
  55.0 0.0 copy-start.3
  55.0 0.7 shard_map.54
  55.6 10.6 %all-to-all-start.2 = ((f32[12,3,128]{2,1,0:T(4,128)}), f32[12,3,128]{2,1,0:T(4,128)S(1)}, u32[]{:S(2)}, u32[]{:S(2)}) async-start(f32[12,3,128]{2,1,0:T(4,128)} %shard_map.54), calls=%async_computation.2 | async-start | bytes 49152 | tf_op jit(solution)/shard_map/all_to_all | solution.py:172
  66.3 0.0 collective-permute-done.high_ref
  66.3 0.0 copy-done.3
  66.3 1.3 %shard_map.55 = bf16[64,8,128]{2,1,0:T(8,128)(2,1)} custom-call(bf16[64,8,128]{2,1,0:T(8,128)(2,1)S(1)} %bitcast.10, bf16[128,8,128]{2,1,0:T(8,128)(2,1)S(1)} %collective-permute-done.high_ref, bf16[384,1024]{1,0:T(8,128)(2,1)S(1)} %get-tuple-element.19.moved_ref, f32[192,1024]{1,0:T(8,128)S(1)} %get-tuple-element.22.sum_ref, ...), custom_call_target="tpu_custom_call" | custom-call | flops 2000000000 | bytes 2000000 | tf_op jit(solution)/shard_map/pallas_call | solution.py:144
  67.6 7.6 %all-to-all-done.2 = f32[12,3,128]{2,1,0:T(4,128)S(1)} async-done(((f32[12,3,128]{2,1,0:T(4,128)}), f32[12,3,128]{2,1,0:T(4,128)S(1)}, u32[]{:S(2)}, u32[]{:S(2)}) %all-to-all-start.2) | async-done | bytes 18464 | tf_op jit(solution)/shard_map/all_to_all | solution.py:172
  75.2 0.7 dynamic_slice.3
  (3 shorter events, 0.1 us)
Async XLA Ops:
  0.6 12.6 %collective-permute-start.2 = (bf16[128,8,128]{2,1,0:T(8,128)(2,1)}, bf16[128,8,128]{2,1,0:T(8,128)(2,1)S(1)}, u32[]{:S(2)}, u32[]{:S(2)}) collective-permute-start(bf16[128,8,128]{2,1,0:T(8,128)(2,1)} %bitcast.6), channel_id=1, source_target_pairs={{0,32},{32,64},{64,96},{96,128},{128,160},{160,192},{192,224},{224... | collective-permute-start | bytes 786440 | tf_op jit(solution)/shard_map/ppermute | solution.py:186
  5.5 7.8 %collective-permute-start.1 = (bf16[64,8,128]{2,1,0:T(8,128)(2,1)}, bf16[64,8,128]{2,1,0:T(8,128)(2,1)S(1)}, u32[]{:S(2)}, u32[]{:S(2)}) collective-permute-start(bf16[64,8,128]{2,1,0:T(8,128)(2,1)} %bitcast.8), channel_id=1, source_target_pairs={{0,32},{32,64},{64,96},{96,128},{128,160},{160,192},{192,224},{224... | collective-permute-start | bytes 393224 | tf_op jit(solution)/shard_map/ppermute | solution.py:187
  9.5 1.0 %copy-start = (bf16[27,64,128]{2,1,0:T(8,128)(2,1)S(1)}, bf16[27,64,128]{2,1,0:T(8,128)(2,1)}, u32[]{:S(2)}) copy-start(bf16[27,64,128]{2,1,0:T(8,128)(2,1)} %w_ref.1) | copy-start | bytes 1327108
  10.5 0.9 %copy-start.1 = (bf16[1,128,1,8,128]{4,3,2,1,0:T(8,128)(2,1)S(1)}, bf16[1,128,1,8,128]{4,3,2,1,0:T(8,128)(2,1)}, u32[]{:S(2)}) copy-start(bf16[1,128,1,8,128]{4,3,2,1,0:T(8,128)(2,1)} %param.4) | copy-start | bytes 786436
  11.4 0.9 %copy-start.2 = (bf16[1,64,1,8,128]{4,3,2,1,0:T(8,128)(2,1)S(1)}, bf16[1,64,1,8,128]{4,3,2,1,0:T(8,128)(2,1)}, u32[]{:S(2)}) copy-start(bf16[1,64,1,8,128]{4,3,2,1,0:T(8,128)(2,1)} %param.3) | copy-start | bytes 393220
  35.9 19.0 %all-to-all-start.1 = ((f16[16,40,128]{2,1,0:T(8,128)(2,1)}), f16[16,40,128]{2,1,0:T(8,128)(2,1)S(1)}, u32[]{:S(2)}, u32[]{:S(2)}) async-start(f16[16,40,128]{2,1,0:T(8,128)(2,1)} %convert_element_type.14), calls=%async_computation.1 | async-start | bytes 327680 | tf_op jit(solution)/shard_map/all_to_all | solution.py:172
  45.4 20.8 %collective-permute-start = (bf16[128,8,128]{2,1,0:T(8,128)(2,1)S(1)}, bf16[128,8,128]{2,1,0:T(8,128)(2,1)S(1)}, u32[]{:S(2)}, u32[]{:S(2)}) collective-permute-start(bf16[128,8,128]{2,1,0:T(8,128)(2,1)S(1)} %shard_map.51), channel_id=1, source_target_pairs={{32,0},{64,32},{96,64},{128,96},{160,128},{192,160},{224,192},{256... | collective-permute-start | bytes 786440 | tf_op jit(solution)/shard_map/ppermute | solution.py:210
  55.0 11.3 %copy-start.3 = (bf16[1,64,1,8,128]{4,3,2,1,0:T(8,128)(2,1)S(1)}, bf16[1,64,1,8,128]{4,3,2,1,0:T(8,128)(2,1)}, u32[]{:S(2)}) copy-start(bf16[1,64,1,8,128]{4,3,2,1,0:T(8,128)(2,1)} %param.3) | copy-start | bytes 393220
  55.6 19.6 %all-to-all-start.2 = ((f32[12,3,128]{2,1,0:T(4,128)}), f32[12,3,128]{2,1,0:T(4,128)S(1)}, u32[]{:S(2)}, u32[]{:S(2)}) async-start(f32[12,3,128]{2,1,0:T(4,128)} %shard_map.54), calls=%async_computation.2 | async-start | bytes 49152 | tf_op jit(solution)/shard_map/all_to_all | solution.py:172
